TPU v7x, 256 devices: a whole 4x4x8 slice. The times are simulated.
256 devices in a mesh: dp: 32 (over y, z), rows: 8 (over x, core).
Axes of the slice: x: 4, y: 4, z: 8, core: 2. Of those that a mesh axis runs over, the one named last changes fastest.
Arguments:
- item_ids: int32 [32768], P(('dp', 'rows')), may hold values from 0 to 4095, as said below
- lengths: int32 [256, 4], P(('dp', 'rows')), may hold values from 1 to 64, 128 in all within a row
- item_table: bfloat16 [4096, 512], P('rows'), may hold values from -6 to 6
- in_weight: bfloat16 [512, 2048], replicated, may hold values from -0.25 to 0.25
- out_weight: bfloat16 [512, 512], replicated, may hold values from -0.25 to 0.25
- grad_out: bfloat16 [32768, 512], P(('dp', 'rows')), may hold values from -6 to 6
Outputs:
- mixed_rows: bfloat16 [32768, 512], P(('dp', 'rows'))
- table_grad: float32 [4096, 512], P('rows')
Inputs may be any that keep to these rules, and one draw needn't show every extreme that they name: `item_ids`: table shard s holds items s*512 to (s+1)*512 - 1. The 128 IDs of each block fall at most 32 times into any one shard, and exactly 32 times into one shard of every block. `lengths`: each row sums to 128, and its largest entry is exactly 64.
All inputs are finite; a program needn't handle non-finite values.
Results may differ from a plain program's by a relative error of at most 0.0064.
Values may be sent and summed in bfloat16 or wider, within the bound.
A program may use at most 64 MiB of HBM per device.

v0:
```python
import jax
import jax.numpy as jnp
from jax import lax
from jax.sharding import PartitionSpec as P

HEADS = 8
MAXLEN = 64


EPS = 1e-06
EXACT = lax.Precision.HIGHEST


def filled_up(lines, devices):
    spare = -len(lines) % devices
    return jnp.pad(lines, [(0, spare)] + [(0, 0)] * (lines.ndim - 1))


def in_order(blocks, dim):
    blocks = jnp.moveaxis(blocks, 0, dim)
    dims = blocks.shape
    return blocks.reshape(*dims[:dim], dims[dim] * dims[dim + 1], *dims[dim + 2 :])


def from_everyone(array, axis):
    devices = lax.axis_size(axis)
    return lax.all_to_all(
        jnp.broadcast_to(array[None], (devices, *array.shape)), axis, 0, 0, tiled=True
    )


def gather_directly(array, axis, dim):
    return in_order(from_everyone(array, axis), dim)


def in_blocks(array, dim, devices):
    before, after = (array.shape[:dim], array.shape[dim + 1 :])
    return jnp.moveaxis(array.reshape(*before, devices, -1, *after), dim, 0)


def sent_and_summed(array, axis, dim):
    blocks = in_blocks(array, dim, lax.axis_size(axis))
    arrived = lax.all_to_all(blocks, axis, split_axis=0, concat_axis=0, tiled=True)
    return arrived.astype(jnp.float32).sum(axis=0)


def nested_sum(array, axes):
    lines = array.reshape(-1, array.shape[-1])
    padded = filled_up(lines, lax.axis_size(axes))
    whole = gather_directly(sent_and_summed(padded, axes, 0).astype(jnp.bfloat16), axes, 0)
    return lax.slice_in_dim(whole, 0, len(lines)).reshape(array.shape).astype(jnp.float32)


def contract_last(left, right):
    return lax.dot_general(
        left, right, (((1,), (1,)), ((), ())), preferred_element_type=jnp.float32
    )


def contract_first(left, right, precision):
    return lax.dot_general(
        left,
        right,
        (((0,), (0,)), ((), ())),
        precision=precision,
        preferred_element_type=jnp.float32,
    )


def batched(form, left, right):
    return jnp.einsum(form, left, right, preferred_element_type=jnp.float32)


def hstu_layer(rows, lengths_row, cotangent, in_weight, out_weight):
    tokens, features = rows.shape
    head_count = HEADS
    head_size = features // head_count
    score_scale = head_size ** (-0.5)
    input_wide = rows.astype(jnp.float32)
    row_scale = lax.rsqrt(jnp.mean(input_wide * input_wide, axis=-1, keepdims=True) + EPS)
    unit_input = input_wide * row_scale
    normed = unit_input.astype(jnp.bfloat16)
    projected = jnp.dot(normed, in_weight, preferred_element_type=jnp.float32)
    sigmoid_proj = jax.nn.sigmoid(projected)
    activated = projected * sigmoid_proj
    gate_units = activated[:, :features]
    value_heads = (
        activated[:, features : 2 * features]
        .astype(jnp.bfloat16)
        .reshape(tokens, head_count, head_size)
    )
    query_heads = (
        activated[:, 2 * features : 3 * features]
        .astype(jnp.bfloat16)
        .reshape(tokens, head_count, head_size)
    )
    key_heads = (
        activated[:, 3 * features :].astype(jnp.bfloat16).reshape(tokens, head_count, head_size)
    )
    places = jnp.arange(tokens, dtype=jnp.int32)
    user_ends = jnp.cumsum(lengths_row)
    user_of = jnp.sum((places[:, None] >= user_ends[None, :]).astype(jnp.int32), axis=1)
    allowed = (
        (user_of[:, None] == user_of[None, :]) & (places[None, :] <= places[:, None])
    ).astype(jnp.float32)
    scores = batched("qhd,khd->hqk", query_heads, key_heads) * score_scale
    sigmoid_score = jax.nn.sigmoid(scores)
    weights = (scores * sigmoid_score * allowed / MAXLEN).astype(jnp.bfloat16)
    attended = batched("hqk,khd->qhd", weights, value_heads).reshape(tokens, features)
    attended_scale = lax.rsqrt(jnp.mean(attended * attended, axis=-1, keepdims=True) + EPS)
    unit_output = attended * attended_scale
    gated_out = (unit_output * gate_units).astype(jnp.bfloat16)
    layer_out = (
        input_wide + jnp.dot(gated_out, out_weight, preferred_element_type=jnp.float32)
    ).astype(jnp.bfloat16)
    grad_gated = contract_last(cotangent, out_weight)
    grad_gate = grad_gated * unit_output
    grad_unit = grad_gated * gate_units
    grad_att = attended_scale * (
        grad_unit - unit_output * jnp.mean(grad_unit * unit_output, axis=-1, keepdims=True)
    )
    grad_att = grad_att.astype(jnp.bfloat16).reshape(tokens, head_count, head_size)
    grad_weights = batched("qhd,khd->hqk", grad_att, value_heads)
    grad_values = batched("hqk,qhd->khd", weights, grad_att).reshape(tokens, features)
    grad_scores = (
        grad_weights
        * allowed
        / MAXLEN
        * sigmoid_score
        * (1.0 + scores * (1.0 - sigmoid_score))
        * score_scale
    )
    grad_scores = grad_scores.astype(jnp.bfloat16)
    grad_queries = batched("hqk,khd->qhd", grad_scores, key_heads).reshape(tokens, features)
    grad_keys = batched("hqk,qhd->khd", grad_scores, query_heads).reshape(tokens, features)
    grad_activated = jnp.concatenate([grad_gate, grad_values, grad_queries, grad_keys], axis=1)
    grad_pre = (grad_activated * sigmoid_proj * (1.0 + projected * (1.0 - sigmoid_proj))).astype(
        jnp.bfloat16
    )
    grad_normed = contract_last(grad_pre, in_weight)
    grad_rows = cotangent.astype(jnp.float32) + row_scale * (
        grad_normed - unit_input * jnp.mean(grad_normed * unit_input, axis=-1, keepdims=True)
    )
    return (layer_out, grad_rows)


def shards(item_ids, lengths, item_table, in_weight, out_weight, grad_out):
    tokens = item_ids.shape[0]
    features = item_table.shape[1]
    shard_rows = item_table.shape[0]
    owners = lax.axis_size("rows")
    capacity = 2 * tokens // owners
    holder = item_ids // shard_rows
    offset = item_ids - holder * shard_rows
    member = (holder[:, None] == jnp.arange(owners, dtype=jnp.int32)[None, :]).astype(jnp.int32)
    running = jnp.cumsum(member, axis=0)
    slot_index = jnp.sum(running * member, axis=1) - 1
    flat_slot = holder * capacity + slot_index
    slot_match = flat_slot[:, None] == jnp.arange(owners * capacity, dtype=jnp.int32)[None, :]
    slot_float = slot_match.astype(jnp.float32)
    slot_half = slot_match.astype(jnp.bfloat16)
    offset_column = offset.astype(jnp.float32)[:, None]
    send_ids = (
        contract_first(slot_float, offset_column, EXACT).astype(jnp.int32).reshape(owners, capacity)
    )
    requested = lax.all_to_all(send_ids, "rows", split_axis=0, concat_axis=0, tiled=True)
    found_rows = jnp.take(item_table, requested, axis=0)
    returned = lax.all_to_all(found_rows, "rows", split_axis=0, concat_axis=0, tiled=True)
    fetched, requested = (returned, requested)
    picked = jnp.dot(
        slot_half, fetched.reshape(owners * capacity, features), preferred_element_type=jnp.float32
    )
    rows = picked.astype(jnp.bfloat16)
    layer_out, grad_rows = hstu_layer(rows, lengths[0], grad_out, in_weight, out_weight)
    outgoing = contract_first(slot_float, grad_rows, EXACT).reshape(owners, capacity, features)
    incoming = lax.all_to_all(
        outgoing.astype(jnp.bfloat16), "rows", split_axis=0, concat_axis=0, tiled=True
    ).astype(outgoing.dtype)
    target_match = (
        requested.reshape(owners * capacity)[:, None]
        == jnp.arange(shard_rows, dtype=jnp.int32)[None, :]
    ).astype(jnp.float32)
    shard_grad = contract_first(target_match, incoming.reshape(owners * capacity, features), EXACT)
    table_grad = nested_sum(shard_grad.astype(jnp.bfloat16), "dp")
    return (layer_out, table_grad)


def solution(mesh):
    placed = (
        P(("dp", "rows")),
        P(("dp", "rows"), None),
        P("rows", None),
        P(),
        P(),
        P(("dp", "rows"), None),
    )
    return jax.shard_map(
        shards,
        mesh=mesh,
        in_specs=placed,
        out_specs=(P(("dp", "rows"), None), P("rows", None)),
        check_vma=False,
    )
```

profile of v0, /device:TPU:32, one launch (start us, length us, event | category | flops | bytes accessed | tf_op | source)
XLA Modules:
  0.0 108.5 jit_solution(7560622282138548896)
XLA Ops:
  2.6 0.8 fusion.25
  4.1 4.3 %all-to-all-start = ((s32[8,1,32]{2,1,0:T(1,128)}), s32[8,1,32]{2,1,0:T(1,128)S(1)}, u32[]{:S(2)}, u32[]{:S(2)}) async-start(s32[8,1,32]{2,1,0:T(1,128)} %all_to_all.22), calls=%async_computation | async-start | bytes 8192 | tf_op jit(solution)/shard_map/all_to_all | solution.py:166
  9.3 4.4 %all-to-all-done = s32[8,1,32]{2,1,0:T(1,128)S(1)} async-done(((s32[8,1,32]{2,1,0:T(1,128)}), s32[8,1,32]{2,1,0:T(1,128)S(1)}, u32[]{:S(2)}, u32[]{:S(2)}) %all-to-all-start) | async-done | bytes 1056 | tf_op jit(solution)/shard_map/all_to_all | solution.py:166
  13.8 2.3 %gather_fusion = bf16[256,512]{1,0:T(8,128)(2,1)S(1)} fusion(bf16[512,512]{1,0:T(8,128)(2,1)} %param.8, s32[1024]{0:T(1024)S(1)} %pad_clamp_fusion), kind=kCustom, calls=%fused_computation | custom fusion | bytes 525312 | tf_op jit(solution)/shard_map/jit(_take)/gather | solution.py:167
  16.9 3.4 %all-to-all-start.1 = ((bf16[8,32,512]{2,1,0:T(8,128)(2,1)}), bf16[8,32,512]{2,1,0:T(8,128)(2,1)S(1)}, u32[]{:S(2)}, u32[]{:S(2)}) async-start(bf16[8,32,512]{2,1,0:T(8,128)(2,1)} %broadcast_select_fusion), calls=%async_computation.1 | async-start | bytes 524288 | tf_op jit(solution)/shard_map/all_to_all | solution.py:168
  21.1 6.6 %all-to-all-done.1 = bf16[8,32,512]{2,1,0:T(8,128)(2,1)S(1)} async-done(((bf16[8,32,512]{2,1,0:T(8,128)(2,1)}), bf16[8,32,512]{2,1,0:T(8,128)(2,1)S(1)}, u32[]{:S(2)}, u32[]{:S(2)}) %all-to-all-start.1) | async-done | bytes 262176 | tf_op jit(solution)/shard_map/all_to_all | solution.py:168
  28.1 1.8 %fusion.40 = (bf16[128,2048]{1,0:T(8,128)(2,1)S(1)}, f32[128,2048]{1,0:T(8,128)}, f32[128,2048]{1,0:T(8,128)}) fusion(bf16[512,2048]{1,0:T(8,128)(2,1)S(1)} %copy-done, f32[128,512]{1,0:T(8,128)S(1)} %get-tuple-element.10, f32[128]{0:T(128)S(1)} %add_rsqrt_fusion.1), kind=kOutput, calls=%fused_computation.81 | convolution fusion | flops 269877248 | bytes 4981248 | tf_op jit(solution)/shard_map/dot_general | solution.py:83
  30.4 2.1 %multiply_convert_fusion = (bf16[8,128,128]{2,1,0:T(8,128)(2,1)S(1)}, f32[8,128,128]{2,1,0:T(8,128)}) fusion(f32[128,128]{1,0:T(8,128)} %fusion.31, bf16[128,8,64]{0,2,1:T(8,128)(2,1)S(1)} %bitcast.66, bf16[128,8,64]{0,2,1:T(8,128)(2,1)S(1)} %bitcast.64), kind=kOutput, calls=%fused_computation.21 | convolution fusion | flops 17825792 | bytes 1114112 | tf_op jit(solution)/shard_map/qhd,khd->hqk/dot_general | solution.py:71
  32.5 1.0 fusion.12
  33.5 1.1 copy.39
  34.6 1.4 %multiply_reduce_fusion.1 = (f32[128]{0:T(128)S(1)}, f32[128,512]{1,0:T(8,128)S(1)}) fusion(f32[128,512]{1,0:T(8,128)S(1)} %copy.39, f32[128]{0:T(128)S(1)} %add_rsqrt_fusion, f32[128,2048]{1,0:T(8,128)} %get-tuple-element.3, bf16[128,512]{1,0:T(8,128)(2,1)} %param.11, bf16[512,512]{1,0:T(8,128)(2,1)S(1)} %copy-done.1), kind=kOutput, calls=%fused_computation.32 | convolution fusion | flops 67370880 | bytes 1442816 | tf_op jit(solution)/shard_map/dot_general | solution.py:55
  36.0 1.8 %multiply_multiply_fusion = (f32[128,512]{1,0:T(8,128)}, bf16[128,512]{1,0:T(8,128)(2,1)S(1)}) fusion(f32[128,512]{1,0:T(8,128)S(1)} %get-tuple-element.17, f32[128,512]{1,0:T(8,128)S(1)} %copy.39, f32[128]{0:T(128)S(1)} %add_rsqrt_fusion, f32[128]{0:T(128)S(1)} %broadcast_multiply_fusion.1, f32[128,2048]{1,0:T(8,128)} %get-tuple-element.3), kind=kLoop, calls=%fused_computation.41 | loop fusion | flops 458752 | bytes 1180672 | tf_op jit(solution)/shard_map/mul | solution.py:117
  38.1 1.5 %fusion.4 = bf16[8,128,128]{2,1,0:T(8,128)(2,1)S(1)} fusion(bf16[128,8,64]{0,2,1:T(8,128)(2,1)S(1)} %bitcast.69, bf16[128,8,64]{0,2,1:T(8,128)(2,1)} %bitcast.71, f32[8,128,128]{2,1,0:T(8,128)} %get-tuple-element.13, f32[128,128]{1,0:T(8,128)} %fusion.31), kind=kOutput, calls=%fused_computation.9 | convolution fusion | flops 18350080 | bytes 1114112 | tf_op jit(solution)/shard_map/qhd,khd->hqk/dot_general | solution.py:71
  40.1 0.9 copy.41
  41.2 2.3 %multiply_reduce_fusion = (f32[128]{0:T(128)S(1)}, f32[128,512]{1,0:T(8,128)S(1)}) fusion(f32[128,512]{1,0:T(8,128)S(1)} %get-tuple-element.10, f32[128]{0:T(128)S(1)} %add_rsqrt_fusion.1, bf16[512,2048]{1,0:T(8,128)(2,1)S(1)} %copy-done, f32[128,512]{1,0:T(8,128)S(1)} %copy.43, f32[128,512]{1,0:T(8,128)S(1)} %copy.42, f32[128,512]{1,0:T(8,128)} %copy.41, ...), kind=kOutput, calls=%fused_computation.30 | convolution fusion | flops 271777664 | bytes 4719616 | tf_op jit(solution)/shard_map/dot_general | solution.py:55
  43.6 1.2 %convolution_convert_fusion.1 = bf16[256,512]{1,0:T(8,128)(2,1)} fusion(f32[128,512]{1,0:T(8,128)S(1)} %get-tuple-element.19, bf16[128,512]{1,0:T(8,128)(2,1)S(1)} %copy-done.4, f32[128,512]{1,0:T(8,128)S(1)} %get-tuple-element.10, f32[128]{0:T(128)S(1)} %broadcast_multiply_fusion, f32[128]{0:T(128)S(1)} %add_rsqrt_fusion.1, s32[128]{0:T(128)S(1)} %add_add_fusion), kind=kOutput, calls=%fused_computation.8 | convolution fusion | flops 201883648 | bytes 919040 | tf_op jit(solution)/shard_map/dot_general | solution.py:61
  44.8 3.4 %all-to-all-start.2 = ((bf16[8,32,512]{2,1,0:T(8,128)(2,1)}), bf16[8,32,512]{2,1,0:T(8,128)(2,1)S(1)}, u32[]{:S(2)}, u32[]{:S(2)}) async-start(bf16[8,32,512]{2,1,0:T(8,128)(2,1)} %bitcast.20), calls=%async_computation.2 | async-start | bytes 524288 | tf_op jit(solution)/shard_map/all_to_all | solution.py:176
  49.5 6.2 %all-to-all-done.2 = bf16[8,32,512]{2,1,0:T(8,128)(2,1)S(1)} async-done(((bf16[8,32,512]{2,1,0:T(8,128)(2,1)}), bf16[8,32,512]{2,1,0:T(8,128)(2,1)S(1)}, u32[]{:S(2)}, u32[]{:S(2)}) %all-to-all-start.2) | async-done | bytes 262176 | tf_op jit(solution)/shard_map/all_to_all | solution.py:176
  56.1 28.4 %all_to_all.35 = bf16[32,16,512]{2,1,0:T(8,128)(2,1)S(1)} all-to-all(bf16[32,16,512]{2,1,0:T(8,128)(2,1)S(1)} %bitcast.56), channel_id=1, replica_groups=mesh['dp'=32,'rows'=8] {'dp'}, dimensions={0} | all-to-all | bytes 1048576 | tf_op jit(solution)/shard_map/all_to_all | solution.py:43
  84.6 0.9 broadcast_in_dim.14
  85.4 4.8 %all-to-all-start.4 = ((bf16[32,16,512]{2,1,0:T(8,128)(2,1)}), bf16[32,16,512]{2,1,0:T(8,128)(2,1)S(1)}, u32[]{:S(2)}, u32[]{:S(2)}) async-start(bf16[32,16,512]{2,1,0:T(8,128)(2,1)} %broadcast_in_dim.14), calls=%async_computation.4 | async-start | bytes 1048576 | tf_op jit(solution)/shard_map/all_to_all | solution.py:27
  90.3 2.1 %fusion.5 = bf16[128,512]{1,0:T(8,128)(2,1)} fusion(f32[128,512]{1,0:T(8,128)S(1)} %get-tuple-element.10, bf16[512,512]{1,0:T(8,128)(2,1)} %param.10, f32[128,2048]{1,0:T(8,128)} %get-tuple-element.3, f32[128,512]{1,0:T(8,128)S(1)} %copy.39, f32[128]{0:T(128)S(1)} %add_rsqrt_fusion), kind=kOutput, calls=%fused_computation.11 | convolution fusion | flops 67436544 | bytes 1442304 | tf_op jit(solution)/shard_map/dot_general | solution.py:114
  92.3 15.0 %all-to-all-done.4 = bf16[32,16,512]{2,1,0:T(8,128)(2,1)S(1)} async-done(((bf16[32,16,512]{2,1,0:T(8,128)(2,1)}), bf16[32,16,512]{2,1,0:T(8,128)(2,1)S(1)}, u32[]{:S(2)}, u32[]{:S(2)}) %all-to-all-start.4) | async-done | bytes 524320 | tf_op jit(solution)/shard_map/all_to_all | solution.py:27
  107.4 1.1 %bitcast_convert_fusion = f32[512,512]{1,0:T(8,128)} fusion(bf16[32,16,512]{2,1,0:T(8,128)(2,1)S(1)} %all-to-all-done.4), kind=kLoop, calls=%fused_computation.19 | loop fusion | flops 262144 | bytes 1572864 | tf_op jit(solution)/shard_map/convert_element_type | solution.py:51
  (47 shorter events, 8.7 us)
Async XLA Ops:
  0.6 27.4 %copy-start = (bf16[512,2048]{1,0:T(8,128)(2,1)S(1)}, bf16[512,2048]{1,0:T(8,128)(2,1)}, u32[]{:S(2)}) copy-start(bf16[512,2048]{1,0:T(8,128)(2,1)} %param.9) | copy-start | bytes 6291460
  4.1 9.5 %all-to-all-start = ((s32[8,1,32]{2,1,0:T(1,128)}), s32[8,1,32]{2,1,0:T(1,128)S(1)}, u32[]{:S(2)}, u32[]{:S(2)}) async-start(s32[8,1,32]{2,1,0:T(1,128)} %all_to_all.22), calls=%async_computation | async-start | bytes 8192 | tf_op jit(solution)/shard_map/all_to_all | solution.py:166
  16.9 10.9 %all-to-all-start.1 = ((bf16[8,32,512]{2,1,0:T(8,128)(2,1)}), bf16[8,32,512]{2,1,0:T(8,128)(2,1)S(1)}, u32[]{:S(2)}, u32[]{:S(2)}) async-start(bf16[8,32,512]{2,1,0:T(8,128)(2,1)} %broadcast_select_fusion), calls=%async_computation.1 | async-start | bytes 524288 | tf_op jit(solution)/shard_map/all_to_all | solution.py:168
  30.2 3.3 %copy-start.2 = (bf16[128,512]{0,1:T(8,128)(2,1)}, bf16[128,512]{0,1:T(8,128)(2,1)S(1)}, u32[]{:S(2)}) copy-start(bf16[128,512]{0,1:T(8,128)(2,1)S(1)} %copy.37) | copy-start | bytes 393220
  30.2 4.4 %copy-start.1 = (bf16[512,512]{1,0:T(8,128)(2,1)S(1)}, bf16[512,512]{1,0:T(8,128)(2,1)}, u32[]{:S(2)}) copy-start(bf16[512,512]{1,0:T(8,128)(2,1)} %param.10) | copy-start | bytes 1572868
  30.3 3.1 %copy-start.5 = (bf16[128,512]{0,1:T(8,128)(2,1)}, bf16[128,512]{0,1:T(8,128)(2,1)S(1)}, u32[]{:S(2)}) copy-start(bf16[128,512]{0,1:T(8,128)(2,1)S(1)} %copy.36) | copy-start | bytes 393220
  37.8 1.8 %copy-start.3 = (bf16[128,512]{0,1:T(8,128)(2,1)S(1)}, bf16[128,512]{0,1:T(8,128)(2,1)}, u32[]{:S(2)}) copy-start(bf16[128,512]{0,1:T(8,128)(2,1)} %copy-done.2) | copy-start | bytes 393220
  41.2 2.4 %copy-start.4 = (bf16[128,512]{1,0:T(8,128)(2,1)S(1)}, bf16[128,512]{1,0:T(8,128)(2,1)}, u32[]{:S(2)}) copy-start(bf16[128,512]{1,0:T(8,128)(2,1)} %param.11) | copy-start | bytes 393220
  44.8 10.8 %all-to-all-start.2 = ((bf16[8,32,512]{2,1,0:T(8,128)(2,1)}), bf16[8,32,512]{2,1,0:T(8,128)(2,1)S(1)}, u32[]{:S(2)}, u32[]{:S(2)}) async-start(bf16[8,32,512]{2,1,0:T(8,128)(2,1)} %bitcast.20), calls=%async_computation.2 | async-start | bytes 524288 | tf_op jit(solution)/shard_map/all_to_all | solution.py:176
  85.4 21.9 %all-to-all-start.4 = ((bf16[32,16,512]{2,1,0:T(8,128)(2,1)}), bf16[32,16,512]{2,1,0:T(8,128)(2,1)S(1)}, u32[]{:S(2)}, u32[]{:S(2)}) async-start(bf16[32,16,512]{2,1,0:T(8,128)(2,1)} %broadcast_in_dim.14), calls=%async_computation.4 | async-start | bytes 1048576 | tf_op jit(solution)/shard_map/all_to_all | solution.py:27
where the time goes:
time: 109 us
  waiting for transfers between devices  32.2 us (30%)
  blocking collectives  28.4 us (26%)
  starting transfers between devices  16 us (15%)
  matrix products  15.7 us (14%)
  other arithmetic  8.03 us (7%)
  local copies, waits for them, and re-layouts  7.29 us (7%)
    all_to_all x1, blocking collectives, sent_and_summed(): lax.all_to_all(blocks, axis, split_axis=0, concat_axis=0, tiled=True)  28.4 us
    all_to_all x1, waiting for transfers between devices, from_everyone(): lax.all_to_all(jnp.broadcast_to(array[None], (devices, *array.shape)), ax...  15 us
    all_to_all x1, waiting for transfers between devices, shards(): lax.all_to_all(found_rows, 'rows', split_axis=0, concat_axis=0, tiled=True)  6.64 us
    all_to_all x1, waiting for transfers between devices, shards(): lax.all_to_all(outgoing.astype(jnp.bfloat16), 'rows', split_axis=0, conca...  6.17 us
    dot_general x6, matrix products, batched(): return jnp.einsum(form, left, right, preferred_element_type=jnp.float32)  5.28 us
    all_to_all x1, starting transfers between devices, from_everyone(): lax.all_to_all(jnp.broadcast_to(array[None], (devices, *array.shape)), ax...  4.84 us
    all_to_all x1, waiting for transfers between devices, shards(): lax.all_to_all(send_ids, 'rows', split_axis=0, concat_axis=0, tiled=True)  4.39 us
    all_to_all x1, starting transfers between devices, shards(): lax.all_to_all(send_ids, 'rows', split_axis=0, concat_axis=0, tiled=True)  4.3 us
  transfers between devices with their start and end apart: 4, of which 4 were waited for; matrix products, arithmetic and copies ran while one was open for 5% of the time, Pallas kernels for 0%

commit v1 on v0

v1 whole, which is shorter than its diff:
```python
import functools

import jax
import jax.numpy as jnp
from jax import lax
from jax.experimental import pallas as pl
from jax.experimental.pallas import tpu as pltpu
from jax.sharding import PartitionSpec as P

HEADS = 8
MAXLEN = 64
EPS = 1e-06
NY = 4
CHUNKS = 2
F32 = jnp.float32
BF16 = jnp.bfloat16
I32 = jnp.int32
ROW_ORDER = (4, 3, 5, 2, 6, 1, 7)
Y_ORDER = (2, 1, 3)
Z_ORDER = (4, 3, 5, 2, 6, 1, 7)


def mm(left, right):
    return jnp.dot(left, right, preferred_element_type=F32)


def mm_last(left, right):
    return lax.dot_general(left, right, (((1,), (1,)), ((), ())), preferred_element_type=F32)


def mm_first(left, right):
    return lax.dot_general(left, right, (((0,), (0,)), ((), ())), preferred_element_type=F32)


def iota(shape, dim):
    return lax.broadcasted_iota(I32, shape, dim)


def kernel(
    owners,
    nz,
    ids_hbm,
    lens_hbm,
    table_hbm,
    win_hbm,
    wout_hbm,
    cot_hbm,
    out_ref,
    tg_ref,
    ids_v,
    ids_all,
    lens_s,
    tab,
    win,
    wout,
    cot_v,
    rsend,
    fetched,
    at_s,
    pt_s,
    p_s,
    gg_s,
    allow_s,
    dact_s,
    gate_s,
    vqk_s,
    w_s,
    dsw_s,
    att_s,
    gpre_s,
    gsend,
    grecv,
    ysend,
    yrecv,
    zsend,
    zrecv,
    local_sem,
    ids_ss,
    ids_rs,
    row_ss,
    row_rs,
    x_ss,
    x_rs,
    y_ss,
    y_rs,
    z_ss,
    z_rs,
    az_ss,
    az_rs,
    ay_ss,
    ay_rs,
):
    tokens = ids_v.shape[1]
    shard_rows, features = tab.shape
    cap = rsend.shape[1]
    me = lax.axis_index("rows")
    dp = lax.axis_index("dp")
    yi = dp // nz
    zi = lax.rem(dp, nz)

    def row_dev(k):
        return (dp, lax.rem(me + owners - k, owners))

    def y_of(k):
        return lax.rem(yi + k, NY)

    def z_of(k):
        return lax.rem(zi + k, nz)

    def y_dev(k):
        return (y_of(k) * nz + zi, me)

    def z_dev(k):
        return (yi * nz + z_of(k), me)

    def rcopy(src, dst, ss, rs, dev):
        return pltpu.make_async_remote_copy(
            src_ref=src,
            dst_ref=dst,
            send_sem=ss,
            recv_sem=rs,
            device_id=dev,
            device_id_type=pl.DeviceIdType.MESH,
        )

    ids_load = pltpu.make_async_copy(ids_hbm, ids_v, local_sem.at[0])
    lens_load = pltpu.make_async_copy(lens_hbm, lens_s, local_sem.at[1])
    tab_load = pltpu.make_async_copy(table_hbm, tab, local_sem.at[2])
    win_load = pltpu.make_async_copy(win_hbm, win, local_sem.at[3])
    wout_load = pltpu.make_async_copy(wout_hbm, wout, local_sem.at[4])
    cot_load = pltpu.make_async_copy(cot_hbm, cot_v, local_sem.at[5])
    ids_load.start()
    lens_load.start()

    barrier = pltpu.get_barrier_semaphore()
    peers = 0
    for k in Z_ORDER:
        pl.semaphore_signal(barrier, inc=1, device_id=z_dev(k), device_id_type=pl.DeviceIdType.MESH)
        peers += 1
    for k in Y_ORDER:
        pl.semaphore_signal(barrier, inc=1, device_id=y_dev(k), device_id_type=pl.DeviceIdType.MESH)
        peers += 1
    for k in ROW_ORDER:
        pl.semaphore_signal(
            barrier, inc=1, device_id=row_dev(k), device_id_type=pl.DeviceIdType.MESH
        )
        peers += 1
    tab_load.start()
    cot_load.start()
    wout_load.start()
    win_load.start()
    ids_load.wait()
    pl.semaphore_wait(barrier, peers)

    ids_copies = []
    for k in ROW_ORDER:
        back = owners - k
        c = rcopy(ids_v, ids_all.at[back], ids_ss.at[back], ids_rs.at[back], row_dev(k))
        c.start()
        ids_copies.append(c)

    ids = ids_v[...]
    before = (iota((tokens, tokens), 0) < iota((tokens, tokens), 1)).astype(BF16)
    rel = lax.rem(me + owners - ids // shard_rows, owners)
    memb = rel == iota((owners, tokens), 0)
    rank = mm(memb.astype(BF16), before)
    slot_row = jnp.sum(
        jnp.where(memb, rank + (iota((owners, tokens), 0) * cap).astype(F32), 0.0),
        axis=0,
        keepdims=True,
    )
    slot_ids = iota((owners * cap, tokens), 0).astype(F32)
    pt_s[...] = (slot_ids == slot_row).astype(BF16)
    diag = iota((tokens, tokens), 0) == iota((tokens, tokens), 1)
    slot_col = jnp.sum(
        jnp.where(diag, jnp.broadcast_to(slot_row, (tokens, tokens)), 0.0), axis=1, keepdims=True
    )
    p_s[...] = (iota((tokens, owners * cap), 1).astype(F32) == slot_col).astype(BF16)

    lens_load.wait()
    ends = []
    total = lens_s[0, 0]
    ends.append(total)
    for u in range(1, lens_s.shape[1]):
        total = total + lens_s[0, u]
        ends.append(total)
    ti = iota((tokens, tokens), 0)
    tj = iota((tokens, tokens), 1)
    ui = sum((ti >= e).astype(I32) for e in ends)
    uj = sum((tj >= e).astype(I32) for e in ends)
    allow_s[...] = jnp.where((ui == uj) & (tj <= ti), 1.0 / MAXLEN, 0.0)

    for c in ids_copies:
        c.wait_recv()
    lo = me * shard_rows
    ids_mat = jnp.concatenate([ids] + [ids_all[k] for k in range(1, owners)], axis=0)
    mine = (ids_mat >= lo) & (ids_mat < lo + shard_rows)
    mrank = mm(mine.astype(BF16), before)
    key = jnp.where(mine, mrank, -1.0)
    off1 = jnp.where(mine, (ids_mat - lo + 1).astype(F32), 0.0)
    slots = iota((cap, tokens), 0).astype(F32)
    cols = []
    for k in range(owners):
        cols.append(
            jnp.sum(
                jnp.where(slots == key[k : k + 1, :], off1[k : k + 1, :], 0.0),
                axis=1,
                keepdims=True,
            )
        )
    off_col = jnp.concatenate(cols, axis=0) - 1.0
    pick = (iota((owners * cap, shard_rows), 1).astype(F32) == off_col).astype(BF16)
    tab_load.wait()
    found = mm(pick, tab[...]).astype(BF16)
    rsend[...] = found.reshape(owners, cap, features)
    row_copies = []
    for k in ROW_ORDER:
        c = rcopy(
            rsend.at[k], fetched.at[owners - k], row_ss.at[owners - k], row_rs.at[owners - k], row_dev(k)
        )
        c.start()
        row_copies.append(c)
    fetched[0] = rsend[0]

    at_s[...] = pick.T
    cot_load.wait()
    wout_load.wait()
    gg_s[...] = mm_last(cot_v[...], wout[...])
    win_load.wait()

    for c in row_copies:
        c.wait_recv()
    x = mm(p_s[...], fetched[...].reshape(owners * cap, features))
    row_scale = lax.rsqrt(jnp.mean(x * x, axis=-1, keepdims=True) + EPS)
    unit_x = x * row_scale
    normed = unit_x.astype(BF16)
    width = 256
    for j in range(4 * features // width):
        here = slice(j * width, (j + 1) * width)
        p = mm(normed, win[:, here])
        s = jax.nn.sigmoid(p)
        a = p * s
        dact_s[:, here] = s * (1.0 + p * (1.0 - s))
        if j * width < features:
            gate_s[:, here] = a
        else:
            vqk_s[:, j * width - features : (j + 1) * width - features] = a.astype(BF16)

    pair = 2 * (features // HEADS)
    low = iota((tokens, pair), 1) < pair // 2
    allow = allow_s[...]
    allow2 = jnp.concatenate([allow, allow], axis=0)
    zero = jnp.zeros((tokens, pair), BF16)

    def split(b):
        return jnp.concatenate([jnp.where(low, b, zero), jnp.where(low, zero, b)], axis=0)

    def beside(b):
        return jnp.concatenate([b[:tokens], b[tokens:]], axis=1)

    score_scale = (features // HEADS) ** (-0.5)
    for g in range(HEADS // 2):
        v2 = vqk_s[:, g * pair : (g + 1) * pair]
        q2 = vqk_s[:, features + g * pair : features + (g + 1) * pair]
        k2 = vqk_s[:, 2 * features + g * pair : 2 * features + (g + 1) * pair]
        s = mm_last(split(q2), k2) * score_scale
        sg = jax.nn.sigmoid(s)
        w = (s * sg * allow2).astype(BF16)
        w_s[g] = w
        dsw_s[g] = allow2 * sg * (1.0 + s * (1.0 - sg)) * score_scale
        att_s[:, g * pair : (g + 1) * pair] = mm(beside(w), split(v2))

    att = att_s[...]
    att_scale = lax.rsqrt(jnp.mean(att * att, axis=-1, keepdims=True) + EPS)
    unit_o = att * att_scale
    gate = gate_s[...]
    gg = gg_s[...]
    grad_unit = gg * gate
    ga = att_scale * (grad_unit - unit_o * jnp.mean(grad_unit * unit_o, axis=-1, keepdims=True))
    ga = ga.astype(BF16)
    gpre_s[:, :features] = (gg * unit_o * dact_s[:, :features]).astype(BF16)
    gated = (unit_o * gate).astype(BF16)
    for g in range(HEADS // 2):
        v_at = slice(features + g * pair, features + (g + 1) * pair)
        q_at = slice(2 * features + g * pair, 2 * features + (g + 1) * pair)
        k_at = slice(3 * features + g * pair, 3 * features + (g + 1) * pair)
        v2 = vqk_s[:, g * pair : (g + 1) * pair]
        q2 = vqk_s[:, features + g * pair : features + (g + 1) * pair]
        k2 = vqk_s[:, 2 * features + g * pair : 2 * features + (g + 1) * pair]
        gas = split(ga[:, g * pair : (g + 1) * pair])
        gw = mm_last(gas, v2)
        ds = (gw * dsw_s[g]).astype(BF16)
        gv = mm_first(w_s[g], gas)
        gq = mm(beside(ds), split(k2))
        gk = mm_first(ds, split(q2))
        gpre_s[:, v_at] = (gv * dact_s[:, v_at]).astype(BF16)
        gpre_s[:, q_at] = (gq * dact_s[:, q_at]).astype(BF16)
        gpre_s[:, k_at] = (gk * dact_s[:, k_at]).astype(BF16)
    gn = mm_last(gpre_s[...], win[...])
    grad_rows = cot_v[...].astype(F32) + row_scale * (
        gn - unit_x * jnp.mean(gn * unit_x, axis=-1, keepdims=True)
    )
    outgoing = mm(pt_s[...], grad_rows.astype(BF16)).astype(BF16)
    gsend[...] = outgoing.reshape(owners, cap, features)
    cw = features // CHUNKS
    x_copies, y_copies, z_copies, az_copies, ay_copies = [], [], [], [], []
    for c in range(CHUNKS):
        at = pl.ds(c * cw, cw)
        for k in ROW_ORDER:
            d = rcopy(
                gsend.at[k, :, at],
                grecv.at[owners - k, :, at],
                x_ss.at[c, owners - k],
                x_rs.at[c, owners - k],
                row_dev(k),
            )
            d.start()
            x_copies.append(d)
    grecv[0] = gsend[0]

    out_ref[...] = (x + mm(gated, wout[...])).astype(BF16)

    peer_count = owners - 1
    for c in range(CHUNKS):
        here = slice(c * cw, (c + 1) * cw)
        at = pl.ds(c * cw, cw)
        for d in x_copies[c * peer_count : (c + 1) * peer_count]:
            d.wait_recv()
        dense = mm(at_s[...], grecv[:, :, here].reshape(owners * cap, cw)).astype(BF16)
        ysend[:, :, here] = dense.reshape(NY, shard_rows // NY, cw)
        for k in Y_ORDER:
            d = rcopy(
                ysend.at[y_of(k), :, at], yrecv.at[k, :, at], y_ss.at[c, k], y_rs.at[c, k], y_dev(k)
            )
            d.start()
            y_copies.append(d)
    for c in range(CHUNKS):
        here = slice(c * cw, (c + 1) * cw)
        at = pl.ds(c * cw, cw)
        for d in y_copies[c * (NY - 1) : (c + 1) * (NY - 1)]:
            d.wait_recv()
        part = ysend[yi, :, here].astype(F32)
        for k in range(1, NY):
            part = part + yrecv[k, :, here].astype(F32)
        zsend[:, :, here] = part.astype(BF16).reshape(nz, shard_rows // (NY * nz), cw)
        for k in Z_ORDER:
            d = rcopy(
                zsend.at[z_of(k), :, at], zrecv.at[k, :, at], z_ss.at[c, k], z_rs.at[c, k], z_dev(k)
            )
            d.start()
            z_copies.append(d)
    for c in range(CHUNKS):
        here = slice(c * cw, (c + 1) * cw)
        at = pl.ds(c * cw, cw)
        for d in z_copies[c * (nz - 1) : (c + 1) * (nz - 1)]:
            d.wait_recv()
        part = zsend[zi, :, here].astype(F32)
        for k in range(1, nz):
            part = part + zrecv[k, :, here].astype(F32)
        tg_ref[yi, zi, :, here] = part.astype(BF16)
        for k in Z_ORDER:
            d = rcopy(
                tg_ref.at[yi, zi, :, at],
                tg_ref.at[yi, zi, :, at],
                az_ss.at[c, k],
                az_rs.at[c, k],
                z_dev(k),
            )
            d.start()
            az_copies.append(d)
    for c in range(CHUNKS):
        at = pl.ds(c * cw, cw)
        for k in Z_ORDER:
            came = lax.rem(zi + nz - k, nz)
            rcopy(
                tg_ref.at[yi, came, :, at],
                tg_ref.at[yi, came, :, at],
                az_ss.at[c, k],
                az_rs.at[c, k],
                z_dev(k),
            ).wait_recv()
        for k in Y_ORDER:
            d = rcopy(
                tg_ref.at[yi, :, :, at],
                tg_ref.at[yi, :, :, at],
                ay_ss.at[c, k],
                ay_rs.at[c, k],
                y_dev(k),
            )
            d.start()
            ay_copies.append(d)
    for c in range(CHUNKS):
        at = pl.ds(c * cw, cw)
        for k in Y_ORDER:
            came = lax.rem(yi + NY - k, NY)
            rcopy(
                tg_ref.at[came, :, :, at],
                tg_ref.at[came, :, :, at],
                ay_ss.at[c, k],
                ay_rs.at[c, k],
                y_dev(k),
            ).wait_recv()
    for d in ids_copies + row_copies + x_copies + y_copies + z_copies + az_copies + ay_copies:
        d.wait_send()


def solution(mesh):
    owners = mesh.shape["rows"]
    nz = mesh.shape["dp"] // NY

    def shards(item_ids, lengths, item_table, in_weight, out_weight, grad_out):
        tokens = item_ids.shape[0]
        shard_rows, features = item_table.shape
        cap = 2 * tokens // owners
        piece = shard_rows // (NY * nz)
        dma = pltpu.SemaphoreType.DMA
        any_spec = pl.BlockSpec(memory_space=pl.ANY)
        vmem = pl.BlockSpec(memory_space=pltpu.VMEM)
        heads2 = HEADS // 2
        mixed, table_grad = pl.pallas_call(
            functools.partial(kernel, owners, nz),
            name="hstu",
            out_shape=(
                jax.ShapeDtypeStruct((tokens, features), BF16),
                jax.ShapeDtypeStruct((NY, nz, piece, features), BF16),
            ),
            in_specs=[any_spec] * 6,
            out_specs=(vmem, vmem),
            scratch_shapes=[
                pltpu.VMEM((1, tokens), I32),
                pltpu.VMEM((owners, 1, tokens), I32),
                pltpu.SMEM(lengths.shape, I32),
                pltpu.VMEM((shard_rows, features), BF16),
                pltpu.VMEM(in_weight.shape, BF16),
                pltpu.VMEM(out_weight.shape, BF16),
                pltpu.VMEM((tokens, features), BF16),
                pltpu.VMEM((owners, cap, features), BF16),
                pltpu.VMEM((owners, cap, features), BF16),
                pltpu.VMEM((shard_rows, owners * cap), BF16),
                pltpu.VMEM((owners * cap, tokens), BF16),
                pltpu.VMEM((tokens, owners * cap), BF16),
                pltpu.VMEM((tokens, features), F32),
                pltpu.VMEM((tokens, tokens), F32),
                pltpu.VMEM((tokens, 4 * features), F32),
                pltpu.VMEM((tokens, features), F32),
                pltpu.VMEM((tokens, 3 * features), BF16),
                pltpu.VMEM((heads2, 2 * tokens, tokens), BF16),
                pltpu.VMEM((heads2, 2 * tokens, tokens), F32),
                pltpu.VMEM((tokens, features), F32),
                pltpu.VMEM((tokens, 4 * features), BF16),
                pltpu.VMEM((owners, cap, features), BF16),
                pltpu.VMEM((owners, cap, features), BF16),
                pltpu.VMEM((NY, shard_rows // NY, features), BF16),
                pltpu.VMEM((NY, shard_rows // NY, features), BF16),
                pltpu.VMEM((nz, piece, features), BF16),
                pltpu.VMEM((nz, piece, features), BF16),
                dma((6,)),
                dma((owners,)),
                dma((owners,)),
                dma((owners,)),
                dma((owners,)),
                dma((CHUNKS, owners)),
                dma((CHUNKS, owners)),
                dma((CHUNKS, NY)),
                dma((CHUNKS, NY)),
                dma((CHUNKS, nz)),
                dma((CHUNKS, nz)),
                dma((CHUNKS, nz)),
                dma((CHUNKS, nz)),
                dma((CHUNKS, NY)),
                dma((CHUNKS, NY)),
            ],
            compiler_params=pltpu.CompilerParams(
                collective_id=0, has_side_effects=True, vmem_limit_bytes=40 * 1024 * 1024
            ),
        )(
            item_ids.reshape(1, tokens),
            lengths,
            item_table,
            in_weight,
            out_weight,
            grad_out,
        )
        return mixed, table_grad.reshape(shard_rows, features).astype(F32)

    return jax.shard_map(
        shards,
        mesh=mesh,
        in_specs=(
            P(("dp", "rows")),
            P(("dp", "rows"), None),
            P("rows", None),
            P(),
            P(),
            P(("dp", "rows"), None),
        ),
        out_specs=(P(("dp", "rows"), None), P("rows", None)),
        check_vma=False,
    )
```

time: 109 us -> 57.4 us (0.53)
  Pallas kernels: 0 us -> 48.1 us
  waiting for transfers between devices: 32.2 us -> 0 us
  blocking collectives: 28.4 us -> 0 us
  starting transfers between devices: 16 us -> 0 us
  matrix products: 15.7 us -> 0 us
  other arithmetic: 8.03 us -> 1.14 us
    pallas_call x0 -> x1, Pallas kernels: none -> 48.1 us  [shards(): pl.pallas_call(functools.partial(kernel, owners, nz), name='hstu', out_sh...]
    all_to_all x4 -> x0, waiting for transfers between devices: 32.2 us -> none  [the longest x1 15 us: from_everyone(): lax.all_to_all(jnp.broadcast_to(array[None], (devices, *array.shape)), ax...]
    all_to_all x1 -> x0, blocking collectives: 28.4 us -> none  [sent_and_summed(): lax.all_to_all(blocks, axis, split_axis=0, concat_axis=0, tiled=True)]
    all_to_all x4 -> x0, starting transfers between devices: 16 us -> none  [the longest x1 4.84 us: from_everyone(): lax.all_to_all(jnp.broadcast_to(array[None], (devices, *array.shape)), ax...]
    dot_general x14 -> x0, matrix products: 15.7 us -> none  [the longest x6 5.28 us: batched(): return jnp.einsum(form, left, right, preferred_element_type=jnp.float32)]
    unnamed x12 -> x13, local copies, waits for them, and re-layouts: 0.04 us -> 6.53 us
    gather x1 -> x0, local copies, waits for them, and re-layouts: 2.32 us -> none  [shards(): found_rows = jnp.take(item_table, requested, axis=0)]
    reshape x4 -> x0, local copies, waits for them, and re-layouts: 2.21 us -> none  [the longest x1 1.08 us: hstu_layer(): batched('hqk,khd->qhd', weights, value_heads).reshape(tokens, features)]
  transfers between devices with their start and end apart: 4 -> 0, of which waited for: 4 -> 0; matrix products, arithmetic and copies ran while one was open for 5% -> 0% of each run, Pallas kernels for 0% -> 0%
where the time goes in v1:
time: 57.4 us; the launch traced here: 56.4 us
  Pallas kernels  48.1 us (84%)
  local copies, waits for them, and re-layouts  6.53 us (11%)
  other arithmetic  1.14 us (2%)
  between operations  0.65 us (1%)
    pallas_call x1, Pallas kernels, shards(): pl.pallas_call(functools.partial(kernel, owners, nz), name='hstu', out_sh...  48.1 us
    unnamed x13, local copies, waits for them, and re-layouts  6.53 us

profile of v1, /device:TPU:32, one launch (start us, length us, event | category | flops | bytes accessed | tf_op | source)
XLA Modules:
  0.0 56.4 jit_solution(13342577596049483567)
XLA Ops:
  0.6 0.0 copy-start
  0.6 1.6 %copy-done = bf16[512,2048]{1,0:T(8,128)(2,1)S(1)} copy-done((bf16[512,2048]{1,0:T(8,128)(2,1)S(1)}, bf16[512,2048]{1,0:T(8,128)(2,1)}, u32[]{:S(2)}) %copy-start) | copy-done | bytes 2097176
  2.2 0.0 copy-start.1
  2.2 1.0 %copy-done.1 = bf16[512,512]{1,0:T(8,128)(2,1)S(1)} copy-done((bf16[512,512]{1,0:T(8,128)(2,1)S(1)}, bf16[512,512]{1,0:T(8,128)(2,1)}, u32[]{:S(2)}) %copy-start.1) | copy-done | bytes 524312
  3.3 0.0 copy-start.2
  3.3 1.0 %copy-done.2 = bf16[512,512]{1,0:T(8,128)(2,1)S(1)} copy-done((bf16[512,512]{1,0:T(8,128)(2,1)S(1)}, bf16[512,512]{1,0:T(8,128)(2,1)}, u32[]{:S(2)}) %copy-start.2) | copy-done | bytes 524312
  4.3 0.0 copy-start.3
  4.3 0.9 %copy-done.3 = bf16[128,512]{1,0:T(8,128)(2,1)S(1)} copy-done((bf16[128,512]{1,0:T(8,128)(2,1)S(1)}, bf16[128,512]{1,0:T(8,128)(2,1)}, u32[]{:S(2)}) %copy-start.3) | copy-done | bytes 131096
  5.2 0.0 copy-start.4
  5.2 0.7 %copy-done.4 = s32[128]{0:T(128)S(1)} copy-done((s32[128]{0:T(128)S(1)}, s32[128]{0:T(128)}, u32[]{:S(2)}) %copy-start.4) | copy-done | bytes 536
  5.9 0.0 copy-start.5
  5.9 0.7 %copy-done.5 = s32[1,4]{1,0:T(1,128)S(1)} copy-done((s32[1,4]{1,0:T(1,128)S(1)}, s32[1,4]{1,0:T(1,128)}, u32[]{:S(2)}) %copy-start.5) | copy-done | bytes 40
  6.5 48.1 %hstu.1 = (bf16[128,512]{1,0:T(8,128)(2,1)S(1)}, bf16[4,8,16,512]{3,2,1,0:T(8,128)(2,1)S(1)}) custom-call(s32[1,128]{1,0:T(1,128)S(1)} %bitcast.4, s32[1,4]{1,0:T(1,128)S(1)} %copy-done.5, bf16[512,512]{1,0:T(8,128)(2,1)S(1)} %copy-done.1, bf16[512,2048]{1,0:T(8,128)(2,1)S(1)} %copy-done, bf16[512,512]{1,0:T(8,128)(2,1)S(1)} %copy-done.2, ...), custom_call_target="tpu_custom_call" | custom-call | tf_op jit(solution)/shard_map/hstu/pallas_call | solution.py:420
  54.6 1.1 %bitcast_convert_fusion = f32[512,512]{1,0:T(8,128)} fusion(bf16[4,8,16,512]{3,2,1,0:T(8,128)(2,1)S(1)} %get-tuple-element.5), kind=kLoop, calls=%fused_computation | loop fusion | flops 262144 | bytes 1572864 | tf_op jit(solution)/shard_map/convert_element_type | solution.py:484
  55.7 0.7 %copy.9 = bf16[128,512]{1,0:T(8,128)(2,1)} copy(bf16[128,512]{1,0:T(8,128)(2,1)S(1)} %get-tuple-element.8) | data formatting | bytes 262144
Async XLA Ops:
  0.6 1.6 %copy-start = (bf16[512,2048]{1,0:T(8,128)(2,1)S(1)}, bf16[512,2048]{1,0:T(8,128)(2,1)}, u32[]{:S(2)}) copy-start(bf16[512,2048]{1,0:T(8,128)(2,1)} %win_hbm.1) | copy-start | bytes 6291460
  2.2 1.0 %copy-start.1 = (bf16[512,512]{1,0:T(8,128)(2,1)S(1)}, bf16[512,512]{1,0:T(8,128)(2,1)}, u32[]{:S(2)}) copy-start(bf16[512,512]{1,0:T(8,128)(2,1)} %table_hbm.1) | copy-start | bytes 1572868
  3.3 1.0 %copy-start.2 = (bf16[512,512]{1,0:T(8,128)(2,1)S(1)}, bf16[512,512]{1,0:T(8,128)(2,1)}, u32[]{:S(2)}) copy-start(bf16[512,512]{1,0:T(8,128)(2,1)} %wout_hbm.1) | copy-start | bytes 1572868
  4.3 0.9 %copy-start.3 = (bf16[128,512]{1,0:T(8,128)(2,1)S(1)}, bf16[128,512]{1,0:T(8,128)(2,1)}, u32[]{:S(2)}) copy-start(bf16[128,512]{1,0:T(8,128)(2,1)} %cot_hbm.1) | copy-start | bytes 393220
  5.2 0.7 %copy-start.4 = (s32[128]{0:T(128)S(1)}, s32[128]{0:T(128)}, u32[]{:S(2)}) copy-start(s32[128]{0:T(128)} %param.6) | copy-start | bytes 1540
  5.9 0.7 %copy-start.5 = (s32[1,4]{1,0:T(1,128)S(1)}, s32[1,4]{1,0:T(1,128)}, u32[]{:S(2)}) copy-start(s32[1,4]{1,0:T(1,128)} %lens_hbm.1) | copy-start | bytes 52

commit v2 on v1

--- a/solution.py
+++ b/solution.py
@@ -12,12 +12,15 @@
 EPS = 1e-06
 NY = 4
 CHUNKS = 2
+DELIVERIES = 4
 F32 = jnp.float32
 BF16 = jnp.bfloat16
 I32 = jnp.int32
 ROW_ORDER = (4, 3, 5, 2, 6, 1, 7)
 Y_ORDER = (2, 1, 3)
-Z_ORDER = (4, 3, 5, 2, 6, 1, 7)
+Z_ORDER = (4, 3, 5, 2, 6, 1, 7, 0)
+Z_RUNS = ((0, 3), (3, 5), (5, 7), (7, 8))
+MESH = pl.DeviceIdType.MESH
 
 
 def mm(left, right):
@@ -74,25 +77,22 @@
     yrecv,
     zsend,
     zrecv,
+    own_s,
     local_sem,
-    ids_ss,
-    ids_rs,
-    row_ss,
-    row_rs,
-    x_ss,
+    send_sem,
+    in_sem,
     x_rs,
-    y_ss,
     y_rs,
-    z_ss,
     z_rs,
-    az_ss,
     az_rs,
-    ay_ss,
-    ay_rs,
+    near_sem,
+    far_sem,
 ):
     tokens = ids_v.shape[1]
     shard_rows, features = tab.shape
     cap = rsend.shape[1]
+    piece = zsend.shape[1]
+    cw = features // CHUNKS
     me = lax.axis_index("rows")
     dp = lax.axis_index("dp")
     yi = dp // nz
@@ -115,13 +115,20 @@
 
     def rcopy(src, dst, ss, rs, dev):
         return pltpu.make_async_remote_copy(
-            src_ref=src,
-            dst_ref=dst,
-            send_sem=ss,
-            recv_sem=rs,
-            device_id=dev,
-            device_id_type=pl.DeviceIdType.MESH,
+            src_ref=src, dst_ref=dst, send_sem=ss, recv_sem=rs, device_id=dev, device_id_type=MESH
         )
+
+    def signal(sem, dev):
+        pl.semaphore_signal(sem, inc=1, device_id=dev, device_id_type=MESH)
+
+    s_ids, s_row, s_x, s_y, s_z, s_az, s_ay = (send_sem.at[i] for i in range(7))
+    in_ids, in_row, in_ay = (in_sem.at[i] for i in range(3))
+
+    def came(ref, sem):
+        rcopy(ref, ref, s_ids, sem, row_dev(1)).wait_recv()
+
+    def gone(ref, sem):
+        rcopy(ref, ref, sem, in_ids, row_dev(1)).wait_send()
 
     ids_load = pltpu.make_async_copy(ids_hbm, ids_v, local_sem.at[0])
     lens_load = pltpu.make_async_copy(lens_hbm, lens_s, local_sem.at[1])
@@ -130,34 +137,28 @@
     wout_load = pltpu.make_async_copy(wout_hbm, wout, local_sem.at[4])
     cot_load = pltpu.make_async_copy(cot_hbm, cot_v, local_sem.at[5])
     ids_load.start()
+
+    barrier = pltpu.get_barrier_semaphore()
+    for k in ROW_ORDER:
+        signal(barrier, row_dev(k))
+    for k in (1, NY - 1):
+        signal(barrier, y_dev(k))
+    for k in (1, nz - 1):
+        signal(barrier, z_dev(k))
+    tab_load.start()
     lens_load.start()
-
-    barrier = pltpu.get_barrier_semaphore()
-    peers = 0
-    for k in Z_ORDER:
-        pl.semaphore_signal(barrier, inc=1, device_id=z_dev(k), device_id_type=pl.DeviceIdType.MESH)
-        peers += 1
-    for k in Y_ORDER:
-        pl.semaphore_signal(barrier, inc=1, device_id=y_dev(k), device_id_type=pl.DeviceIdType.MESH)
-        peers += 1
-    for k in ROW_ORDER:
-        pl.semaphore_signal(
-            barrier, inc=1, device_id=row_dev(k), device_id_type=pl.DeviceIdType.MESH
-        )
-        peers += 1
-    tab_load.start()
     cot_load.start()
     wout_load.start()
     win_load.start()
     ids_load.wait()
-    pl.semaphore_wait(barrier, peers)
-
-    ids_copies = []
+    pl.semaphore_wait(barrier, len(ROW_ORDER) + 4)
+
     for k in ROW_ORDER:
-        back = owners - k
-        c = rcopy(ids_v, ids_all.at[back], ids_ss.at[back], ids_rs.at[back], row_dev(k))
-        c.start()
-        ids_copies.append(c)
+        rcopy(ids_v, ids_all.at[owners - k], s_ids, in_ids, row_dev(k)).start()
+    for k in (1, nz - 1):
+        signal(near_sem, z_dev(k))
+    for k in (1, NY - 1):
+        signal(near_sem, y_dev(k))
 
     ids = ids_v[...]
     before = (iota((tokens, tokens), 0) < iota((tokens, tokens), 1)).astype(BF16)
@@ -190,8 +191,7 @@
     uj = sum((tj >= e).astype(I32) for e in ends)
     allow_s[...] = jnp.where((ui == uj) & (tj <= ti), 1.0 / MAXLEN, 0.0)
 
-    for c in ids_copies:
-        c.wait_recv()
+    came(ids_all.at[pl.ds(1, owners - 1)], in_ids)
     lo = me * shard_rows
     ids_mat = jnp.concatenate([ids] + [ids_all[k] for k in range(1, owners)], axis=0)
     mine = (ids_mat >= lo) & (ids_mat < lo + shard_rows)
@@ -213,23 +213,28 @@
     tab_load.wait()
     found = mm(pick, tab[...]).astype(BF16)
     rsend[...] = found.reshape(owners, cap, features)
-    row_copies = []
     for k in ROW_ORDER:
-        c = rcopy(
-            rsend.at[k], fetched.at[owners - k], row_ss.at[owners - k], row_rs.at[owners - k], row_dev(k)
-        )
-        c.start()
-        row_copies.append(c)
+        rcopy(rsend.at[k], fetched.at[owners - k], s_row, in_row, row_dev(k)).start()
     fetched[0] = rsend[0]
 
-    at_s[...] = pick.T
+    spot = iota((1, shard_rows), 1)
+    run_at = lax.rem(spot // piece, nz)
+    along_z = sum(jnp.where(run_at == i, z, 0) for i, z in enumerate(Z_ORDER))
+    item = (
+        lax.rem(yi + spot // (piece * nz), NY) * (piece * nz)
+        + lax.rem(zi + along_z, nz) * piece
+        + lax.rem(spot, piece)
+    )
+    at_s[...] = (item.astype(F32) == off_col).astype(BF16).T
     cot_load.wait()
     wout_load.wait()
     gg_s[...] = mm_last(cot_v[...], wout[...])
     win_load.wait()
-
-    for c in row_copies:
-        c.wait_recv()
+    pl.semaphore_wait(near_sem, 4)
+    for k in (2, nz - 2):
+        signal(far_sem, z_dev(k))
+
+    came(fetched.at[pl.ds(1, owners - 1)], in_row)
     x = mm(p_s[...], fetched[...].reshape(owners * cap, features))
     row_scale = lax.rsqrt(jnp.mean(x * x, axis=-1, keepdims=True) + EPS)
     unit_x = x * row_scale
@@ -302,106 +307,100 @@
     )
     outgoing = mm(pt_s[...], grad_rows.astype(BF16)).astype(BF16)
     gsend[...] = outgoing.reshape(owners, cap, features)
-    cw = features // CHUNKS
-    x_copies, y_copies, z_copies, az_copies, ay_copies = [], [], [], [], []
     for c in range(CHUNKS):
         at = pl.ds(c * cw, cw)
         for k in ROW_ORDER:
-            d = rcopy(
-                gsend.at[k, :, at],
-                grecv.at[owners - k, :, at],
-                x_ss.at[c, owners - k],
-                x_rs.at[c, owners - k],
-                row_dev(k),
-            )
-            d.start()
-            x_copies.append(d)
+            rcopy(gsend.at[k, :, at], grecv.at[owners - k, :, at], s_x, x_rs.at[c], row_dev(k)).start()
     grecv[0] = gsend[0]
 
     out_ref[...] = (x + mm(gated, wout[...])).astype(BF16)
-
-    peer_count = owners - 1
+    pl.semaphore_wait(far_sem, 2)
+
     for c in range(CHUNKS):
         here = slice(c * cw, (c + 1) * cw)
         at = pl.ds(c * cw, cw)
-        for d in x_copies[c * peer_count : (c + 1) * peer_count]:
-            d.wait_recv()
+        came(grecv.at[pl.ds(1, owners - 1), :, at], x_rs.at[c])
         dense = mm(at_s[...], grecv[:, :, here].reshape(owners * cap, cw)).astype(BF16)
-        ysend[:, :, here] = dense.reshape(NY, shard_rows // NY, cw)
-        for k in Y_ORDER:
-            d = rcopy(
-                ysend.at[y_of(k), :, at], yrecv.at[k, :, at], y_ss.at[c, k], y_rs.at[c, k], y_dev(k)
-            )
-            d.start()
-            y_copies.append(d)
+        ysend[:, :, :, here] = dense.reshape(NY, nz, piece, cw)
+        for r, (p0, p1) in enumerate(Z_RUNS):
+            run = pl.ds(p0, p1 - p0)
+            for k in Y_ORDER:
+                rcopy(
+                    ysend.at[k, run, :, at],
+                    yrecv.at[k, run, :, at],
+                    s_y,
+                    y_rs.at[c * len(Z_RUNS) + r],
+                    y_dev(k),
+                ).start()
     for c in range(CHUNKS):
         here = slice(c * cw, (c + 1) * cw)
         at = pl.ds(c * cw, cw)
-        for d in y_copies[c * (NY - 1) : (c + 1) * (NY - 1)]:
-            d.wait_recv()
-        part = ysend[yi, :, here].astype(F32)
-        for k in range(1, NY):
-            part = part + yrecv[k, :, here].astype(F32)
-        zsend[:, :, here] = part.astype(BF16).reshape(nz, shard_rows // (NY * nz), cw)
-        for k in Z_ORDER:
-            d = rcopy(
-                zsend.at[z_of(k), :, at], zrecv.at[k, :, at], z_ss.at[c, k], z_rs.at[c, k], z_dev(k)
-            )
-            d.start()
-            z_copies.append(d)
+        for r, (p0, p1) in enumerate(Z_RUNS):
+            run = pl.ds(p0, p1 - p0)
+            came(yrecv.at[pl.ds(1, NY - 1), run, :, at], y_rs.at[c * len(Z_RUNS) + r])
+            part = ysend[0, p0:p1, :, here].astype(F32)
+            for k in range(1, NY):
+                part = part + yrecv[k, p0:p1, :, here].astype(F32)
+            if Z_ORDER[p0] == 0:
+                own_s[:, here] = part[0]
+                continue
+            zsend[p0:p1, :, here] = part.astype(BF16)
+            for p in range(p0, p1):
+                rcopy(
+                    zsend.at[p, :, at], zrecv.at[p, :, at], s_z, z_rs.at[c], z_dev(Z_ORDER[p])
+                ).start()
+
+    def along_y(c, z):
+        ref = tg_ref.at[yi, z, :, pl.ds(c * cw, cw)]
+        for k in Y_ORDER:
+            rcopy(ref, ref, s_ay, in_ay, y_dev(k)).start()
+
     for c in range(CHUNKS):
         here = slice(c * cw, (c + 1) * cw)
         at = pl.ds(c * cw, cw)
-        for d in z_copies[c * (nz - 1) : (c + 1) * (nz - 1)]:
-            d.wait_recv()
-        part = zsend[zi, :, here].astype(F32)
-        for k in range(1, nz):
-            part = part + zrecv[k, :, here].astype(F32)
+        came(zrecv.at[pl.ds(0, nz - 1), :, at], z_rs.at[c])
+        part = own_s[:, here]
+        for p in range(nz - 1):
+            part = part + zrecv[p, :, here].astype(F32)
         tg_ref[yi, zi, :, here] = part.astype(BF16)
-        for k in Z_ORDER:
-            d = rcopy(
-                tg_ref.at[yi, zi, :, at],
-                tg_ref.at[yi, zi, :, at],
-                az_ss.at[c, k],
-                az_rs.at[c, k],
-                z_dev(k),
-            )
-            d.start()
-            az_copies.append(d)
+        ref = tg_ref.at[yi, zi, :, at]
+        for r, (p0, p1) in enumerate(Z_RUNS[:-1]):
+            for p in range(p0, p1):
+                rcopy(ref, ref, s_az, az_rs.at[c * 3 + r], z_dev(Z_ORDER[p])).start()
+        along_y(c, zi)
     for c in range(CHUNKS):
         at = pl.ds(c * cw, cw)
-        for k in Z_ORDER:
-            came = lax.rem(zi + nz - k, nz)
-            rcopy(
-                tg_ref.at[yi, came, :, at],
-                tg_ref.at[yi, came, :, at],
-                az_ss.at[c, k],
-                az_rs.at[c, k],
-                z_dev(k),
-            ).wait_recv()
-        for k in Y_ORDER:
-            d = rcopy(
-                tg_ref.at[yi, :, :, at],
-                tg_ref.at[yi, :, :, at],
-                ay_ss.at[c, k],
-                ay_rs.at[c, k],
-                y_dev(k),
-            )
-            d.start()
-            ay_copies.append(d)
-    for c in range(CHUNKS):
-        at = pl.ds(c * cw, cw)
-        for k in Y_ORDER:
-            came = lax.rem(yi + NY - k, NY)
-            rcopy(
-                tg_ref.at[came, :, :, at],
-                tg_ref.at[came, :, :, at],
-                ay_ss.at[c, k],
-                ay_rs.at[c, k],
-                y_dev(k),
-            ).wait_recv()
-    for d in ids_copies + row_copies + x_copies + y_copies + z_copies + az_copies + ay_copies:
-        d.wait_send()
+        for r in (2, 1, 0):
+            p0, p1 = Z_RUNS[r]
+            came(zrecv.at[pl.ds(p0, p1 - p0), :, at], az_rs.at[c * 3 + r])
+            for p in range(p0, p1):
+                along_y(c, lax.rem(zi + nz - Z_ORDER[p], nz))
+    came(tg_ref.at[pl.ds(0, NY - 1)], in_ay)
+    gone(ids_all.at[pl.ds(1, owners - 1)], s_ids)
+    gone(rsend.at[pl.ds(1, owners - 1)], s_row)
+    gone(gsend.at[pl.ds(1, owners - 1)], s_x)
+    gone(ysend.at[pl.ds(1, NY - 1)], s_y)
+    gone(zsend.at[pl.ds(0, nz - 1)], s_z)
+    gone(zsend.at[pl.ds(0, nz - 1)], s_az)
+    gone(tg_ref.at[pl.ds(0, NY - 1)], s_ay)
+
+
+def deliver(mixed_ref, tg_ref, out_hbm, grad_hbm, wide, sem):
+    first = pltpu.make_async_copy(mixed_ref, out_hbm, sem.at[0])
+    first.start()
+    rows = wide.shape[0] // DELIVERIES
+    copies = []
+    for i in range(DELIVERIES):
+        at = slice(i * rows, (i + 1) * rows)
+        wide[at, :] = tg_ref[at, :].astype(F32)
+        c = pltpu.make_async_copy(
+            wide.at[pl.ds(i * rows, rows)], grad_hbm.at[pl.ds(i * rows, rows)], sem.at[i + 1]
+        )
+        c.start()
+        copies.append(c)
+    first.wait()
+    for c in copies:
+        c.wait()
 
 
 def solution(mesh):
@@ -450,38 +449,42 @@
                 pltpu.VMEM((tokens, 4 * features), BF16),
                 pltpu.VMEM((owners, cap, features), BF16),
                 pltpu.VMEM((owners, cap, features), BF16),
-                pltpu.VMEM((NY, shard_rows // NY, features), BF16),
-                pltpu.VMEM((NY, shard_rows // NY, features), BF16),
+                pltpu.VMEM((NY, nz, piece, features), BF16),
+                pltpu.VMEM((NY, nz, piece, features), BF16),
                 pltpu.VMEM((nz, piece, features), BF16),
                 pltpu.VMEM((nz, piece, features), BF16),
+                pltpu.VMEM((piece, features), F32),
                 dma((6,)),
-                dma((owners,)),
-                dma((owners,)),
-                dma((owners,)),
-                dma((owners,)),
-                dma((CHUNKS, owners)),
-                dma((CHUNKS, owners)),
-                dma((CHUNKS, NY)),
-                dma((CHUNKS, NY)),
-                dma((CHUNKS, nz)),
-                dma((CHUNKS, nz)),
-                dma((CHUNKS, nz)),
-                dma((CHUNKS, nz)),
-                dma((CHUNKS, NY)),
-                dma((CHUNKS, NY)),
+                dma((7,)),
+                dma((3,)),
+                dma((CHUNKS,)),
+                dma((CHUNKS * len(Z_RUNS),)),
+                dma((CHUNKS,)),
+                dma((CHUNKS * 3,)),
+                pltpu.SemaphoreType.REGULAR,
+                pltpu.SemaphoreType.REGULAR,
             ],
             compiler_params=pltpu.CompilerParams(
                 collective_id=0, has_side_effects=True, vmem_limit_bytes=40 * 1024 * 1024
             ),
         )(
-            item_ids.reshape(1, tokens),
-            lengths,
-            item_table,
-            in_weight,
-            out_weight,
-            grad_out,
+            *[
+                pltpu.with_memory_space_constraint(v, pltpu.HBM)
+                for v in (item_ids.reshape(1, tokens), lengths, item_table, in_weight, out_weight, grad_out)
+            ]
         )
-        return mixed, table_grad.reshape(shard_rows, features).astype(F32)
+        return pl.pallas_call(
+            deliver,
+            name="deliver",
+            out_shape=(
+                jax.ShapeDtypeStruct((tokens, features), BF16),
+                jax.ShapeDtypeStruct((shard_rows, features), F32),
+            ),
+            in_specs=[vmem, vmem],
+            out_specs=(any_spec, any_spec),
+            scratch_shapes=[pltpu.VMEM((shard_rows, features), F32), dma((DELIVERIES + 1,))],
+            compiler_params=pltpu.CompilerParams(vmem_limit_bytes=8 * 1024 * 1024),
+        )(mixed, table_grad.reshape(shard_rows, features))
 
     return jax.shard_map(
         shards,

time: 57.4 us -> 46.1 us (0.80); the launches traced: 56.4 us -> 45.9 us
  local copies, waits for them, and re-layouts: 6.53 us -> 0 us
  Pallas kernels: 48.1 us -> 45.2 us
  other arithmetic: 1.14 us -> 0 us
    unnamed x13 -> x0, local copies, waits for them, and re-layouts: 6.53 us -> none
    pallas_call x1, Pallas kernels: 48.1 us -> 44.2 us  [shards(): pl.pallas_call(functools.partial(kernel, owners, nz), name='hstu', out_sh...]
    convert_element_type x1 -> x0, other arithmetic: 1.14 us -> none  [shards(): return (mixed, table_grad.reshape(shard_rows, features).astype(F32))]
    pallas_call x0 -> x1, Pallas kernels: none -> 1.05 us  [shards(): pl.pallas_call(deliver, name='deliver', out_shape=(jax.ShapeDtypeStruct((...]
where the time goes in v2:
time: 46.1 us; the launch traced here: 45.9 us
  Pallas kernels  45.2 us (98%)
  between operations  0.64 us (1%)
    pallas_call x1, Pallas kernels, shards(): pl.pallas_call(functools.partial(kernel, owners, nz), name='hstu', out_sh...  44.2 us
    pallas_call x1, Pallas kernels, shards(): pl.pallas_call(deliver, name='deliver', out_shape=(jax.ShapeDtypeStruct((...  1.05 us

profile of v2, /device:TPU:32, one launch (start us, length us, event | category | flops | bytes accessed | tf_op | source)
XLA Modules:
  0.0 45.9 jit_solution(10427594750790482252)
XLA Ops:
  0.6 44.2 %hstu.1 = (bf16[128,512]{1,0:T(8,128)(2,1)S(1)}, bf16[4,8,16,512]{3,2,1,0:T(8,128)(2,1)S(1)}) custom-call(s32[1,128]{1,0:T(1,128)} %bitcast.3, s32[1,4]{1,0:T(1,128)} %lens_hbm.1, bf16[512,512]{1,0:T(8,128)(2,1)} %table_hbm.1, bf16[512,2048]{1,0:T(8,128)(2,1)} %win_hbm.1, bf16[512,512]{1,0:T(8,128)(2,1)} %wout_hbm.1, bf16[128,512]{1,0:T(8,128)(2,1)} %cot_hbm.1), custom_call_target="tpu_custom_call" | custom-call | tf_op jit(solution)/shard_map/hstu/pallas_call | solution.py:419
  44.8 1.0 %deliver.1 = (bf16[128,512]{1,0:T(8,128)(2,1)}, f32[512,512]{1,0:T(8,128)}) custom-call(bf16[128,512]{1,0:T(8,128)(2,1)S(1)} %get-tuple-element.4.mixed_ref, bf16[512,512]{1,0:T(8,128)(2,1)S(1)} %bitcast.2), custom_call_target="tpu_custom_call" | custom-call | tf_op jit(solution)/shard_map/deliver/pallas_call | solution.py:476

commit v3 on v2

--- a/solution.py
+++ b/solution.py
@@ -19,7 +19,8 @@
 ROW_ORDER = (4, 3, 5, 2, 6, 1, 7)
 Y_ORDER = (2, 1, 3)
 Z_ORDER = (4, 3, 5, 2, 6, 1, 7, 0)
-Z_RUNS = ((0, 3), (3, 5), (5, 7), (7, 8))
+Z_FAR, Z_OWN = 0, 7
+Z_RUNS = ((1, 3), (3, 5), (5, 7))
 MESH = pl.DeviceIdType.MESH
 
 
@@ -78,6 +79,8 @@
     zsend,
     zrecv,
     own_s,
+    far_in,
+    own_send,
     local_sem,
     send_sem,
     in_sem,
@@ -85,6 +88,8 @@
     y_rs,
     z_rs,
     az_rs,
+    far_rs,
+    yo_rs,
     near_sem,
     far_sem,
 ):
@@ -316,12 +321,23 @@
     out_ref[...] = (x + mm(gated, wout[...])).astype(BF16)
     pl.semaphore_wait(far_sem, 2)
 
+    runs = len(Z_RUNS)
+
+    def cut(c):
+        return slice(c * cw, (c + 1) * cw), pl.ds(c * cw, cw)
+
     for c in range(CHUNKS):
-        here = slice(c * cw, (c + 1) * cw)
-        at = pl.ds(c * cw, cw)
+        here, at = cut(c)
         came(grecv.at[pl.ds(1, owners - 1), :, at], x_rs.at[c])
         dense = mm(at_s[...], grecv[:, :, here].reshape(owners * cap, cw)).astype(BF16)
         ysend[:, :, :, here] = dense.reshape(NY, nz, piece, cw)
+        rcopy(
+            ysend.at[:, Z_FAR, :, at],
+            far_in.at[:, :, at],
+            s_z,
+            far_rs.at[c],
+            z_dev(Z_ORDER[Z_FAR]),
+        ).start()
         for r, (p0, p1) in enumerate(Z_RUNS):
             run = pl.ds(p0, p1 - p0)
             for k in Y_ORDER:
@@ -329,60 +345,98 @@
                     ysend.at[k, run, :, at],
                     yrecv.at[k, run, :, at],
                     s_y,
-                    y_rs.at[c * len(Z_RUNS) + r],
+                    y_rs.at[c * runs + r],
                     y_dev(k),
                 ).start()
-    for c in range(CHUNKS):
-        here = slice(c * cw, (c + 1) * cw)
-        at = pl.ds(c * cw, cw)
-        for r, (p0, p1) in enumerate(Z_RUNS):
-            run = pl.ds(p0, p1 - p0)
-            came(yrecv.at[pl.ds(1, NY - 1), run, :, at], y_rs.at[c * len(Z_RUNS) + r])
-            part = ysend[0, p0:p1, :, here].astype(F32)
-            for k in range(1, NY):
-                part = part + yrecv[k, p0:p1, :, here].astype(F32)
-            if Z_ORDER[p0] == 0:
-                own_s[:, here] = part[0]
-                continue
-            zsend[p0:p1, :, here] = part.astype(BF16)
-            for p in range(p0, p1):
-                rcopy(
-                    zsend.at[p, :, at], zrecv.at[p, :, at], s_z, z_rs.at[c], z_dev(Z_ORDER[p])
-                ).start()
-
-    def along_y(c, z):
-        ref = tg_ref.at[yi, z, :, pl.ds(c * cw, cw)]
+
+    def over_y(c, r):
+        here, at = cut(c)
+        p0, p1 = Z_RUNS[r]
+        came(yrecv.at[pl.ds(1, NY - 1), pl.ds(p0, p1 - p0), :, at], y_rs.at[c * runs + r])
+        part = ysend[0, p0:p1, :, here].astype(F32)
+        for k in range(1, NY):
+            part = part + yrecv[k, p0:p1, :, here].astype(F32)
+        zsend[p0:p1, :, here] = part.astype(BF16)
+        for p in range(p0, p1):
+            rcopy(
+                zsend.at[p, :, at], zrecv.at[p, :, at], s_z, z_rs.at[c], z_dev(Z_ORDER[p])
+            ).start()
+
+    def over_far(c):
+        here, at = cut(c)
+        came(far_in.at[:, :, at], far_rs.at[c])
+        part = ysend[:, Z_OWN, :, here].astype(F32) + far_in[:, :, here].astype(F32)
+        own_s[:, here] = part[0]
+        own_send[:, :, here] = part.astype(BF16)
         for k in Y_ORDER:
-            rcopy(ref, ref, s_ay, in_ay, y_dev(k)).start()
-
-    for c in range(CHUNKS):
-        here = slice(c * cw, (c + 1) * cw)
-        at = pl.ds(c * cw, cw)
-        came(zrecv.at[pl.ds(0, nz - 1), :, at], z_rs.at[c])
+            rcopy(
+                own_send.at[k, :, at], yrecv.at[k, Z_OWN, :, at], s_y, yo_rs.at[c], y_dev(k)
+            ).start()
+
+    def leave(c):
+        here, at = cut(c)
+        came(yrecv.at[pl.ds(1, NY - 1), Z_OWN, :, at], yo_rs.at[c])
         part = own_s[:, here]
-        for p in range(nz - 1):
+        for k in range(1, NY):
+            part = part + yrecv[k, Z_OWN, :, here].astype(F32)
+        came(zrecv.at[pl.ds(1, nz - 2), :, at], z_rs.at[c])
+        for p in range(1, nz - 1):
             part = part + zrecv[p, :, here].astype(F32)
         tg_ref[yi, zi, :, here] = part.astype(BF16)
         ref = tg_ref.at[yi, zi, :, at]
-        for r, (p0, p1) in enumerate(Z_RUNS[:-1]):
+        for r, (p0, p1) in enumerate(Z_RUNS):
             for p in range(p0, p1):
-                rcopy(ref, ref, s_az, az_rs.at[c * 3 + r], z_dev(Z_ORDER[p])).start()
-        along_y(c, zi)
+                rcopy(ref, ref, s_az, az_rs.at[c * runs + r], z_dev(Z_ORDER[p])).start()
+        for k in Y_ORDER:
+            rcopy(ref, ref, s_ay, yo_rs.at[CHUNKS + c], y_dev(k)).start()
+
+    def to_far(c):
+        here, at = cut(c)
+        came(tg_ref.at[pl.ds(0, NY - 1), 0, :, at], yo_rs.at[CHUNKS + c])
+        ref = tg_ref.at[:, zi, :, at]
+        rcopy(ref, ref, s_az, far_rs.at[CHUNKS + c], z_dev(Z_ORDER[Z_FAR])).start()
+
+    def pass_on(c, r):
+        here, at = cut(c)
+        p0, p1 = Z_RUNS[r]
+        came(zrecv.at[pl.ds(p0, p1 - p0), :, at], az_rs.at[c * runs + r])
+        for p in range(p0, p1):
+            ref = tg_ref.at[yi, lax.rem(zi + nz - Z_ORDER[p], nz), :, at]
+            for k in Y_ORDER:
+                rcopy(ref, ref, s_ay, in_ay, y_dev(k)).start()
+
+    over_y(0, 0)
+    over_y(0, 1)
+    over_y(0, 2)
+    over_y(1, 0)
+    over_far(0)
+    over_y(1, 1)
+    over_y(1, 2)
+    over_far(1)
+    leave(0)
+    leave(1)
+    to_far(0)
+    pass_on(0, 2)
+    pass_on(0, 1)
+    to_far(1)
+    pass_on(1, 2)
+    pass_on(0, 0)
+    pass_on(1, 1)
+    pass_on(1, 0)
     for c in range(CHUNKS):
-        at = pl.ds(c * cw, cw)
-        for r in (2, 1, 0):
-            p0, p1 = Z_RUNS[r]
-            came(zrecv.at[pl.ds(p0, p1 - p0), :, at], az_rs.at[c * 3 + r])
-            for p in range(p0, p1):
-                along_y(c, lax.rem(zi + nz - Z_ORDER[p], nz))
-    came(tg_ref.at[pl.ds(0, NY - 1)], in_ay)
+        here, at = cut(c)
+        came(tg_ref.at[:, 0, :, at], far_rs.at[CHUNKS + c])
+    others = pl.ds(0, nz - 2)
+    came(tg_ref.at[pl.ds(0, NY - 1), others], in_ay)
     gone(ids_all.at[pl.ds(1, owners - 1)], s_ids)
     gone(rsend.at[pl.ds(1, owners - 1)], s_row)
     gone(gsend.at[pl.ds(1, owners - 1)], s_x)
-    gone(ysend.at[pl.ds(1, NY - 1)], s_y)
-    gone(zsend.at[pl.ds(0, nz - 1)], s_z)
-    gone(zsend.at[pl.ds(0, nz - 1)], s_az)
-    gone(tg_ref.at[pl.ds(0, NY - 1)], s_ay)
+    gone(ysend.at[pl.ds(1, NY - 1), pl.ds(0, nz - 1)], s_y)
+    gone(zsend.at[pl.ds(0, nz - 2)], s_z)
+    gone(tg_ref.at[:, 0], s_z)
+    gone(zsend.at[pl.ds(0, nz - 2)], s_az)
+    gone(tg_ref.at[:, 0], s_az)
+    gone(tg_ref.at[pl.ds(0, NY - 1), pl.ds(0, nz - 1)], s_ay)
 
 
 def deliver(mixed_ref, tg_ref, out_hbm, grad_hbm, wide, sem):
@@ -454,13 +508,17 @@
                 pltpu.VMEM((nz, piece, features), BF16),
                 pltpu.VMEM((nz, piece, features), BF16),
                 pltpu.VMEM((piece, features), F32),
+                pltpu.VMEM((NY, piece, features), BF16),
+                pltpu.VMEM((NY, piece, features), BF16),
                 dma((6,)),
                 dma((7,)),
                 dma((3,)),
                 dma((CHUNKS,)),
                 dma((CHUNKS * len(Z_RUNS),)),
                 dma((CHUNKS,)),
-                dma((CHUNKS * 3,)),
+                dma((CHUNKS * len(Z_RUNS),)),
+                dma((2 * CHUNKS,)),
+                dma((2 * CHUNKS,)),
                 pltpu.SemaphoreType.REGULAR,
                 pltpu.SemaphoreType.REGULAR,
             ],

time: 46.1 us -> 45.9 us (level); the launches traced: 45.9 us -> 45.1 us
  Pallas kernels: 45.2 us -> 44.5 us
    pallas_call x1, Pallas kernels: 44.2 us -> 43.4 us  [shards(): pl.pallas_call(functools.partial(kernel, owners, nz), name='hstu', out_sh...]
where the time goes in v3:
time: 45.9 us; the launch traced here: 45.1 us
  Pallas kernels  44.5 us (97%)
  between operations  0.64 us (1%)
    pallas_call x1, Pallas kernels, shards(): pl.pallas_call(functools.partial(kernel, owners, nz), name='hstu', out_sh...  43.4 us
    pallas_call x1, Pallas kernels, shards(): pl.pallas_call(deliver, name='deliver', out_shape=(jax.ShapeDtypeStruct((...  1.05 us

profile of v3, /device:TPU:32, one launch (start us, length us, event | category | flops | bytes accessed | tf_op | source)
XLA Modules:
  0.0 45.1 jit_solution(11522775769122714397)
XLA Ops:
  0.6 43.4 %hstu.1 = (bf16[128,512]{1,0:T(8,128)(2,1)S(1)}, bf16[4,8,16,512]{3,2,1,0:T(8,128)(2,1)S(1)}) custom-call(s32[1,128]{1,0:T(1,128)} %bitcast.3, s32[1,4]{1,0:T(1,128)} %lens_hbm.1, bf16[512,512]{1,0:T(8,128)(2,1)} %table_hbm.1, bf16[512,2048]{1,0:T(8,128)(2,1)} %win_hbm.1, bf16[512,512]{1,0:T(8,128)(2,1)} %wout_hbm.1, bf16[128,512]{1,0:T(8,128)(2,1)} %cot_hbm.1), custom_call_target="tpu_custom_call" | custom-call | tf_op jit(solution)/shard_map/hstu/pallas_call | solution.py:473
  44.1 1.0 %deliver.1 = (bf16[128,512]{1,0:T(8,128)(2,1)}, f32[512,512]{1,0:T(8,128)}) custom-call(bf16[128,512]{1,0:T(8,128)(2,1)S(1)} %get-tuple-element.4.mixed_ref, bf16[512,512]{1,0:T(8,128)(2,1)S(1)} %bitcast.2), custom_call_target="tpu_custom_call" | custom-call | tf_op jit(solution)/shard_map/deliver/pallas_call | solution.py:534

commit v4 on v3

--- a/solution.py
+++ b/solution.py
@@ -36,6 +36,10 @@
     return lax.dot_general(left, right, (((0,), (0,)), ((), ())), preferred_element_type=F32)
 
 
+def sigmoid(v):
+    return 0.5 * jnp.tanh(0.5 * v) + 0.5
+
+
 def iota(shape, dim):
     return lax.broadcasted_iota(I32, shape, dim)
 
@@ -52,10 +56,12 @@
     out_ref,
     tg_ref,
     ids_v,
+    note_s,
     ids_all,
     lens_s,
     tab,
     win,
+    win_t,
     wout,
     cot_v,
     rsend,
@@ -156,25 +162,23 @@
     wout_load.start()
     win_load.start()
     ids_load.wait()
+    ids = ids_v[...]
+    before = (iota((tokens, tokens), 0) < iota((tokens, tokens), 1)).astype(BF16)
+    rel = lax.rem(me + owners - ids // shard_rows, owners)
+    memb = rel == iota((owners, tokens), 0)
+    rank = jnp.sum(jnp.where(memb, mm(memb.astype(BF16), before), 0.0), axis=0, keepdims=True)
+    note_s[0:1, :] = ids
+    note_s[1:2, :] = rank.astype(I32)
     pl.semaphore_wait(barrier, len(ROW_ORDER) + 4)
 
     for k in ROW_ORDER:
-        rcopy(ids_v, ids_all.at[owners - k], s_ids, in_ids, row_dev(k)).start()
+        rcopy(note_s, ids_all.at[owners - k], s_ids, in_ids, row_dev(k)).start()
     for k in (1, nz - 1):
         signal(near_sem, z_dev(k))
     for k in (1, NY - 1):
         signal(near_sem, y_dev(k))
 
-    ids = ids_v[...]
-    before = (iota((tokens, tokens), 0) < iota((tokens, tokens), 1)).astype(BF16)
-    rel = lax.rem(me + owners - ids // shard_rows, owners)
-    memb = rel == iota((owners, tokens), 0)
-    rank = mm(memb.astype(BF16), before)
-    slot_row = jnp.sum(
-        jnp.where(memb, rank + (iota((owners, tokens), 0) * cap).astype(F32), 0.0),
-        axis=0,
-        keepdims=True,
-    )
+    slot_row = rank + (rel * cap).astype(F32)
     slot_ids = iota((owners * cap, tokens), 0).astype(F32)
     pt_s[...] = (slot_ids == slot_row).astype(BF16)
     diag = iota((tokens, tokens), 0) == iota((tokens, tokens), 1)
@@ -198,21 +202,15 @@
 
     came(ids_all.at[pl.ds(1, owners - 1)], in_ids)
     lo = me * shard_rows
-    ids_mat = jnp.concatenate([ids] + [ids_all[k] for k in range(1, owners)], axis=0)
-    mine = (ids_mat >= lo) & (ids_mat < lo + shard_rows)
-    mrank = mm(mine.astype(BF16), before)
-    key = jnp.where(mine, mrank, -1.0)
-    off1 = jnp.where(mine, (ids_mat - lo + 1).astype(F32), 0.0)
-    slots = iota((cap, tokens), 0).astype(F32)
+    slots = iota((cap, tokens), 0)
     cols = []
     for k in range(owners):
-        cols.append(
-            jnp.sum(
-                jnp.where(slots == key[k : k + 1, :], off1[k : k + 1, :], 0.0),
-                axis=1,
-                keepdims=True,
-            )
-        )
+        note = note_s[...] if k == 0 else ids_all[k]
+        asked, place = note[0:1, :], note[1:2, :]
+        mine = (asked >= lo) & (asked < lo + shard_rows)
+        key = jnp.where(mine, place, -1)
+        off1 = jnp.where(mine, asked - lo + 1, 0).astype(F32)
+        cols.append(jnp.sum(jnp.where(slots == key, off1, 0.0), axis=1, keepdims=True))
     off_col = jnp.concatenate(cols, axis=0) - 1.0
     pick = (iota((owners * cap, shard_rows), 1).astype(F32) == off_col).astype(BF16)
     tab_load.wait()
@@ -235,22 +233,23 @@
     wout_load.wait()
     gg_s[...] = mm_last(cot_v[...], wout[...])
     win_load.wait()
+    for j in range(4):
+        win_t[j * features : (j + 1) * features, :] = win[:, j * features : (j + 1) * features].T
     pl.semaphore_wait(near_sem, 4)
     for k in (2, nz - 2):
         signal(far_sem, z_dev(k))
 
     came(fetched.at[pl.ds(1, owners - 1)], in_row)
     x = mm(p_s[...], fetched[...].reshape(owners * cap, features))
+    half = x.astype(BF16)
     row_scale = lax.rsqrt(jnp.mean(x * x, axis=-1, keepdims=True) + EPS)
-    unit_x = x * row_scale
-    normed = unit_x.astype(BF16)
     width = 256
     for j in range(4 * features // width):
         here = slice(j * width, (j + 1) * width)
-        p = mm(normed, win[:, here])
-        s = jax.nn.sigmoid(p)
+        p = mm(half, win[:, here]) * row_scale
+        s = sigmoid(p)
         a = p * s
-        dact_s[:, here] = s * (1.0 + p * (1.0 - s))
+        dact_s[:, here] = s + a * (1.0 - s)
         if j * width < features:
             gate_s[:, here] = a
         else:
@@ -274,19 +273,20 @@
         q2 = vqk_s[:, features + g * pair : features + (g + 1) * pair]
         k2 = vqk_s[:, 2 * features + g * pair : 2 * features + (g + 1) * pair]
         s = mm_last(split(q2), k2) * score_scale
-        sg = jax.nn.sigmoid(s)
+        sg = sigmoid(s)
         w = (s * sg * allow2).astype(BF16)
         w_s[g] = w
         dsw_s[g] = allow2 * sg * (1.0 + s * (1.0 - sg)) * score_scale
         att_s[:, g * pair : (g + 1) * pair] = mm(beside(w), split(v2))
 
     att = att_s[...]
-    att_scale = lax.rsqrt(jnp.mean(att * att, axis=-1, keepdims=True) + EPS)
-    unit_o = att * att_scale
     gate = gate_s[...]
     gg = gg_s[...]
     grad_unit = gg * gate
-    ga = att_scale * (grad_unit - unit_o * jnp.mean(grad_unit * unit_o, axis=-1, keepdims=True))
+    dot_o = jnp.mean(grad_unit * att, axis=-1, keepdims=True)
+    att_scale = lax.rsqrt(jnp.mean(att * att, axis=-1, keepdims=True) + EPS)
+    unit_o = att * att_scale
+    ga = att_scale * (grad_unit - unit_o * (att_scale * dot_o))
     ga = ga.astype(BF16)
     gpre_s[:, :features] = (gg * unit_o * dact_s[:, :features]).astype(BF16)
     gated = (unit_o * gate).astype(BF16)
@@ -306,14 +306,17 @@
         gpre_s[:, v_at] = (gv * dact_s[:, v_at]).astype(BF16)
         gpre_s[:, q_at] = (gq * dact_s[:, q_at]).astype(BF16)
         gpre_s[:, k_at] = (gk * dact_s[:, k_at]).astype(BF16)
-    gn = mm_last(gpre_s[...], win[...])
+    unit_x = x * row_scale
+    gn = mm(gpre_s[...], win_t[...])
     grad_rows = cot_v[...].astype(F32) + row_scale * (
         gn - unit_x * jnp.mean(gn * unit_x, axis=-1, keepdims=True)
     )
-    outgoing = mm(pt_s[...], grad_rows.astype(BF16)).astype(BF16)
-    gsend[...] = outgoing.reshape(owners, cap, features)
+    grad_rows = grad_rows.astype(BF16)
     for c in range(CHUNKS):
+        here = slice(c * cw, (c + 1) * cw)
         at = pl.ds(c * cw, cw)
+        outgoing = mm(pt_s[...], grad_rows[:, here]).astype(BF16)
+        gsend[:, :, here] = outgoing.reshape(owners, cap, cw)
         for k in ROW_ORDER:
             rcopy(gsend.at[k, :, at], grecv.at[owners - k, :, at], s_x, x_rs.at[c], row_dev(k)).start()
     grecv[0] = gsend[0]
@@ -481,10 +484,12 @@
             out_specs=(vmem, vmem),
             scratch_shapes=[
                 pltpu.VMEM((1, tokens), I32),
-                pltpu.VMEM((owners, 1, tokens), I32),
+                pltpu.VMEM((2, tokens), I32),
+                pltpu.VMEM((owners, 2, tokens), I32),
                 pltpu.SMEM(lengths.shape, I32),
                 pltpu.VMEM((shard_rows, features), BF16),
                 pltpu.VMEM(in_weight.shape, BF16),
+                pltpu.VMEM(in_weight.shape[::-1], BF16),
                 pltpu.VMEM(out_weight.shape, BF16),
                 pltpu.VMEM((tokens, features), BF16),
                 pltpu.VMEM((owners, cap, features), BF16),

time: 45.9 us -> 45.5 us (level)
  no operation moved by 1% of the time
where the time goes in v4:
time: 45.5 us; the launch traced here: 45.2 us
  Pallas kernels  44.5 us (98%)
  between operations  0.64 us (1%)
    pallas_call x1, Pallas kernels, shards(): pl.pallas_call(functools.partial(kernel, owners, nz), name='hstu', out_sh...  43.5 us
    pallas_call x1, Pallas kernels, shards(): pl.pallas_call(deliver, name='deliver', out_shape=(jax.ShapeDtypeStruct((...  1.05 us

profile of v4, /device:TPU:32, one launch (start us, length us, event | category | flops | bytes accessed | tf_op | source)
XLA Modules:
  0.0 45.2 jit_solution(13177892854943052287)
XLA Ops:
  0.6 43.5 %hstu.1 = (bf16[128,512]{1,0:T(8,128)(2,1)S(1)}, bf16[4,8,16,512]{3,2,1,0:T(8,128)(2,1)S(1)}) custom-call(s32[1,128]{1,0:T(1,128)} %bitcast.3, s32[1,4]{1,0:T(1,128)} %lens_hbm.1, bf16[512,512]{1,0:T(8,128)(2,1)} %table_hbm.1, bf16[512,2048]{1,0:T(8,128)(2,1)} %win_hbm.1, bf16[512,512]{1,0:T(8,128)(2,1)} %wout_hbm.1, bf16[128,512]{1,0:T(8,128)(2,1)} %cot_hbm.1), custom_call_target="tpu_custom_call" | custom-call | tf_op jit(solution)/shard_map/hstu/pallas_call | solution.py:476
  44.1 1.0 %deliver.1 = (bf16[128,512]{1,0:T(8,128)(2,1)}, f32[512,512]{1,0:T(8,128)}) custom-call(bf16[128,512]{1,0:T(8,128)(2,1)S(1)} %get-tuple-element.4.mixed_ref, bf16[512,512]{1,0:T(8,128)(2,1)S(1)} %bitcast.2), custom_call_target="tpu_custom_call" | custom-call | tf_op jit(solution)/shard_map/deliver/pallas_call | solution.py:539

commit v5 on v4

--- a/solution.py
+++ b/solution.py
@@ -11,7 +11,8 @@
 MAXLEN = 64
 EPS = 1e-06
 NY = 4
-CHUNKS = 2
+CUTS = ((0, 128), (128, 256), (256, 512))
+CHUNKS = len(CUTS)
 DELIVERIES = 4
 F32 = jnp.float32
 BF16 = jnp.bfloat16
@@ -103,7 +104,6 @@
     shard_rows, features = tab.shape
     cap = rsend.shape[1]
     piece = zsend.shape[1]
-    cw = features // CHUNKS
     me = lax.axis_index("rows")
     dp = lax.axis_index("dp")
     yi = dp // nz
@@ -241,12 +241,12 @@
 
     came(fetched.at[pl.ds(1, owners - 1)], in_row)
     x = mm(p_s[...], fetched[...].reshape(owners * cap, features))
-    half = x.astype(BF16)
     row_scale = lax.rsqrt(jnp.mean(x * x, axis=-1, keepdims=True) + EPS)
+    normed = (x * row_scale).astype(BF16)
     width = 256
     for j in range(4 * features // width):
         here = slice(j * width, (j + 1) * width)
-        p = mm(half, win[:, here]) * row_scale
+        p = mm(normed, win[:, here])
         s = sigmoid(p)
         a = p * s
         dact_s[:, here] = s + a * (1.0 - s)
@@ -312,11 +312,11 @@
         gn - unit_x * jnp.mean(gn * unit_x, axis=-1, keepdims=True)
     )
     grad_rows = grad_rows.astype(BF16)
-    for c in range(CHUNKS):
-        here = slice(c * cw, (c + 1) * cw)
-        at = pl.ds(c * cw, cw)
+    for c, (c0, c1) in enumerate(CUTS):
+        here = slice(c0, c1)
+        at = pl.ds(c0, c1 - c0)
         outgoing = mm(pt_s[...], grad_rows[:, here]).astype(BF16)
-        gsend[:, :, here] = outgoing.reshape(owners, cap, cw)
+        gsend[:, :, here] = outgoing.reshape(owners, cap, c1 - c0)
         for k in ROW_ORDER:
             rcopy(gsend.at[k, :, at], grecv.at[owners - k, :, at], s_x, x_rs.at[c], row_dev(k)).start()
     grecv[0] = gsend[0]
@@ -327,13 +327,13 @@
     runs = len(Z_RUNS)
 
     def cut(c):
-        return slice(c * cw, (c + 1) * cw), pl.ds(c * cw, cw)
+        return slice(*CUTS[c]), pl.ds(CUTS[c][0], CUTS[c][1] - CUTS[c][0])
 
     for c in range(CHUNKS):
         here, at = cut(c)
         came(grecv.at[pl.ds(1, owners - 1), :, at], x_rs.at[c])
-        dense = mm(at_s[...], grecv[:, :, here].reshape(owners * cap, cw)).astype(BF16)
-        ysend[:, :, :, here] = dense.reshape(NY, nz, piece, cw)
+        dense = mm(at_s[...], grecv[:, :, here].reshape(owners * cap, -1)).astype(BF16)
+        ysend[:, :, :, here] = dense.reshape(NY, nz, piece, -1)
         rcopy(
             ysend.at[:, Z_FAR, :, at],
             far_in.at[:, :, at],
@@ -408,24 +408,19 @@
             for k in Y_ORDER:
                 rcopy(ref, ref, s_ay, in_ay, y_dev(k)).start()
 
-    over_y(0, 0)
-    over_y(0, 1)
-    over_y(0, 2)
-    over_y(1, 0)
-    over_far(0)
-    over_y(1, 1)
-    over_y(1, 2)
-    over_far(1)
-    leave(0)
-    leave(1)
-    to_far(0)
-    pass_on(0, 2)
-    pass_on(0, 1)
-    to_far(1)
-    pass_on(1, 2)
-    pass_on(0, 0)
-    pass_on(1, 1)
-    pass_on(1, 0)
+    for c in range(CHUNKS):
+        for r in range(runs):
+            over_y(c, r)
+            if c > 0 and r == 0:
+                over_far(c - 1)
+    over_far(CHUNKS - 1)
+    for c in range(CHUNKS):
+        leave(c)
+    steps = [(1.3 * c + 3.0, c, to_far) for c in range(CHUNKS)]
+    for r, late in enumerate((4.6, 3.8, 3.1)):
+        steps += [(1.3 * c + late, c, functools.partial(pass_on, r=r)) for c in range(CHUNKS)]
+    for _, c, step in sorted(steps, key=lambda e: e[:2]):
+        step(c)
     for c in range(CHUNKS):
         here, at = cut(c)
         came(tg_ref.at[:, 0, :, at], far_rs.at[CHUNKS + c])

time: 45.5 us -> 44.7 us (0.982)
  Pallas kernels: 44.5 us -> 43.9 us
    pallas_call x1, Pallas kernels: 43.5 us -> 42.8 us  [shards(): pl.pallas_call(functools.partial(kernel, owners, nz), name='hstu', out_sh...]
where the time goes in v5:
time: 44.7 us; the launch traced here: 44.5 us
  Pallas kernels  43.9 us (98%)
  between operations  0.64 us (1%)
    pallas_call x1, Pallas kernels, shards(): pl.pallas_call(functools.partial(kernel, owners, nz), name='hstu', out_sh...  42.8 us
    pallas_call x1, Pallas kernels, shards(): pl.pallas_call(deliver, name='deliver', out_shape=(jax.ShapeDtypeStruct((...  1.05 us

profile of v5, /device:TPU:32, one launch (start us, length us, event | category | flops | bytes accessed | tf_op | source)
XLA Modules:
  0.0 44.5 jit_solution(12634396273695967648)
XLA Ops:
  0.6 42.8 %hstu.1 = (bf16[128,512]{1,0:T(8,128)(2,1)S(1)}, bf16[4,8,16,512]{3,2,1,0:T(8,128)(2,1)S(1)}) custom-call(s32[1,128]{1,0:T(1,128)} %bitcast.3, s32[1,4]{1,0:T(1,128)} %lens_hbm.1, bf16[512,512]{1,0:T(8,128)(2,1)} %table_hbm.1, bf16[512,2048]{1,0:T(8,128)(2,1)} %win_hbm.1, bf16[512,512]{1,0:T(8,128)(2,1)} %wout_hbm.1, bf16[128,512]{1,0:T(8,128)(2,1)} %cot_hbm.1), custom_call_target="tpu_custom_call" | custom-call | tf_op jit(solution)/shard_map/hstu/pallas_call | solution.py:471
  43.5 1.0 %deliver.1 = (bf16[128,512]{1,0:T(8,128)(2,1)}, f32[512,512]{1,0:T(8,128)}) custom-call(bf16[128,512]{1,0:T(8,128)(2,1)S(1)} %get-tuple-element.4.mixed_ref, bf16[512,512]{1,0:T(8,128)(2,1)S(1)} %bitcast.2), custom_call_target="tpu_custom_call" | custom-call | tf_op jit(solution)/shard_map/deliver/pallas_call | solution.py:534
